TPU v7x, 32 devices: a whole 2x2x4 slice. The times are simulated.
32 devices in a mesh: depth: 2 (over x), lat: 16 (over z, y, core).
Axes of the slice: x: 2, y: 2, z: 4, core: 2. Of those that a mesh axis runs over, the one named last changes fastest.
Arguments:
- displacement: float32 [3, 16, 128, 256], P(None, 'depth', 'lat'), may hold values from -6 to 6
- velocity: float32 [3, 16, 128, 256], P(None, 'depth', 'lat'), may hold values from -6 to 6
- inverse_mass: float32 [16, 128, 256], P('depth', 'lat'), may hold values from 0.5 to 2
- material: int32 [16, 128, 256], P('depth', 'lat'), may hold values from 0 to 7
- dilation_table: float32 [8], replicated, may hold values from 0.5 to 2
- shear_table: float32 [8], replicated, may hold values from 0.5 to 2
- stiffness_pair: float32 [2, 24, 24], replicated, may hold values from -1.5 to 3.5, as said below
- impedance: float32 [3], replicated, may hold values from 0.5 to 2
- bedrock_mask: int32 [128, 256], P('lat'), may hold values 0 or 1
- incident: float32 [6, 3, 128, 256], P(None, None, 'lat'), may hold values from -6 to 6
Outputs:
- new_displacement: float32 [3, 16, 128, 256], P(None, 'depth', 'lat')
- new_velocity: float32 [3, 16, 128, 256], P(None, 'depth', 'lat')
Inputs may be any that keep to these rules, and one draw needn't show every extreme that they name: `stiffness_pair`: symmetric positive definite.
All inputs are finite; a program needn't handle non-finite values. No bound on the sum of `bedrock_mask` on one device may be relied on, other than what follows from the above.
Results may differ from a plain program's by a relative error of at most 0.00016.
Values sent between devices are 32-bit elements; how exact they have to be, the bound alone decides.
No kernel may reach another device: no remote copies, remote signals or barrier semaphores. Data moves between devices by JAX's collectives and lax.ppermute only.
A program may use at most 64 MiB of HBM per device.

v0:
```python
import jax
import jax.numpy as jnp
import numpy as np
from jax import lax
from jax.experimental import pallas as pl
from jax.experimental.pallas import tpu as pltpu
from jax.sharding import PartitionSpec as P

time_step = 0.1
LANES = 128
f32 = jnp.float32
bf16 = jnp.bfloat16


class Plan:
    def __init__(self, mesh, displacement, incident):
        self.D = mesh.shape["depth"]
        self.L = mesh.shape["lat"]
        self.Z = displacement.shape[1] // self.D
        self.Y = displacement.shape[2] // self.L
        self.X = displacement.shape[3]
        self.H = self.X // LANES
        self.T = incident.shape[0]
        T = self.T
        assert T <= self.Z and T <= self.Y and self.Y % 8 == 0
        assert self.X % LANES == 0
        self.hy = T + T % 2
        self.YB = self.Y + 2 * self.hy
        self.PB = self.YB // 2
        self.P0 = self.hy // 2
        self.swap = self.D == 2
        self.ZB = self.Z + (0 if self.D == 1 else T if self.swap else 2 * T)
        self.ZS = self.ZB + 2
        self.YL = -(-self.YB // 8) * 8
        self.gpairs = [-(-(T - 1 - s) // 2) for s in range(T)]
        self.grows = 8 * sum(self.gpairs)
        self.hrow = 4 * self.hy
        self.GL = -(-self.grows // (2 * self.hrow))

    def offset(self, depth):
        if self.D == 1:
            return 0
        return depth * self.T if self.swap else self.T


def g_slots(plan):
    slots, g = [], 0
    for s, n in enumerate(plan.gpairs):
        for k in range(n):
            slots.append((s, k, n, plan.ZB + (8 * g) // (2 * plan.hrow), (8 * g) % (2 * plan.hrow)))
            g += 1
    return slots


def selectors():
    rows = np.zeros((4, 64, 48), np.float32)
    cols = np.zeros((2, 4, 24, 256), np.float32)

    def half(parity, dx):
        return 4 * (dx ^ parity)

    blocks = [(0, 0, 0), (8, 0, 0), (16, 0, 1), (24, 1, 1), (32, 1, 0), (40, 1, 0), (48, 2, 0), (56, 2, 0), (64, 2, 1)]
    for ez in range(2):
        for ey in range(2):
            e = 2 * ez + ey
            for lm in range(2):
                for dz in range(2):
                    for dy in range(2):
                        for dx in range(2):
                            for c in range(3):
                                dof = (4 * dz + 2 * dy + dx) * 3 + c
                                r = half((ey + dy) % 2, dx) + c
                                rows[e, ((lm * 2 + dz) * 2 + dy) * 8 + r, lm * 24 + dof] = 1
            for base, node, low in blocks:
                for zn in range(3):
                    dz, dy = zn - ez, node - ey
                    if dz in (0, 1) and dy in (0, 1):
                        for dx in range(2):
                            for c in range(3):
                                dof = (4 * dz + 2 * dy + dx) * 3 + c
                                cols[low, e, dof, zn * 80 + base + half(node % 2, dx) + c] = 1
    return rows, cols


def matrix_kernel(stiff_ref, rows_ref, cols_ref, out_ref):
    stiff = stiff_ref[...]
    high = stiff.astype(bf16)
    low = (stiff - high.astype(f32)).astype(bf16)
    for e in range(4):
        total = None
        for part, k in ((high, 0), (low, 1)):
            picked = jnp.dot(rows_ref[e], part, preferred_element_type=f32).astype(bf16)
            placed = jnp.dot(picked, cols_ref[k, e], preferred_element_type=f32)
            total = placed if total is None else total + placed
        out_ref[64 * e : 64 * e + 64, :] = total.astype(bf16)


def pack_kernel(plan, scal, u, v, m, mat, mask, inc, xv, g, *zsends):
    Z, Y, H, T = plan.Z, plan.Y, plan.H, plan.T
    for z in range(Z):
        for h in range(H):
            lanes = slice(h * LANES, (h + 1) * LANES)
            for y in range(0, Y, 8):
                rows = slice(y, y + 8)
                for c in range(3):
                    xv[z, h, pl.ds(4 * y + c, 8, stride=4), :] = u[c, z, rows, lanes]
                    xv[z, h, pl.ds(4 * (Y + y) + c, 8, stride=4), :] = v[c, z, rows, lanes]
                xv[z, h, pl.ds(4 * y + 3, 8, stride=4), :] = mat[z, rows, lanes].astype(f32) + 1.0
                xv[z, h, pl.ds(4 * (Y + y) + 3, 8, stride=4), :] = m[z, rows, lanes]
    for h in range(H):
        lanes = slice(h * LANES, (h + 1) * LANES)
        for y in range(0, Y, 8):
            rows = slice(y, y + 8)
            double = 2.0 * mask[rows, lanes].astype(f32)
            for s in range(T):
                for c in range(3):
                    g[s, h, pl.ds(4 * y + c, 8, stride=4), :] = double * inc[s, c, rows, lanes]
                g[s, h, pl.ds(4 * y + 3, 8, stride=4), :] = jnp.zeros((8, LANES), f32)
    for k, zsend in enumerate(zsends):
        if plan.swap:
            first = jnp.where(scal[0] == 0, Z - T, 0)
            first_v = jnp.where(scal[0] == 0, Z - T + 1, 0)
        else:
            first, first_v = (Z - T, Z - T + 1) if k == 0 else (0, 0)
        for i in range(T):
            zsend[i] = xv[first + i, :, : 4 * Y, :]
        for i in range(T - 1):
            zsend[T + i] = xv[first_v + i, :, 4 * Y :, :]


def halo_places(plan, scal):
    if plan.D == 1:
        return []
    if plan.swap:
        top = scal[0] == 0
        return [
            (
                jnp.where(top, plan.Z, 0),
                jnp.where(top, plan.Z, 1),
                jnp.where(top, plan.Z + plan.T - 1, 0),
            )
        ]
    last = plan.T + plan.Z
    return [(0, 1, 0), (last, last, last + plan.T - 1)]


def edge_kernel(plan, scal, xv, g, *refs):
    n = len(refs) - 2
    zrecvs, to_prev, to_next = refs[:n], refs[n], refs[n + 1]
    Y, T, R = plan.Y, plan.T, plan.hrow
    offset = scal[1]
    sides = ((to_prev, 0), (to_next, 4 * Y - R))
    for z in range(plan.Z):
        for out, row in sides:
            out[offset + z, :, :R, :] = xv[z, :, row : row + R, :]
            out[offset + z, :, R:, :] = xv[z, :, 4 * Y + row : 4 * Y + row + R, :]
    for zrecv, (at_u, at_v, lacks) in zip(zrecvs, halo_places(plan, scal)):
        for out, row in sides:
            for i in range(T):
                out[at_u + i, :, :R, :] = zrecv[i, :, row : row + R, :]
            for i in range(T - 1):
                out[at_v + i, :, R:, :] = zrecv[T + i, :, row : row + R, :]
            out[lacks, :, R:, :] = jnp.zeros((plan.H, R, LANES), f32)
    for s, k, n_pairs, layer, row in g_slots(plan):
        to_prev[layer, :, row : row + 8, :] = g[s, :, 8 * k : 8 * k + 8, :]
        at = 4 * Y - 8 * n_pairs + 8 * k
        to_next[layer, :, row : row + 8, :] = g[s, :, at : at + 8, :]


def main_kernel(plan, scal, tables, imp, weights, xv, gown, *refs):
    n = len(refs) - 2 - 2 - 9
    zrecvs = refs[:n]
    from_prev, from_next, out_u, out_v = refs[n : n + 4]
    U, V, DM, lam, mu, G, CI, F, KB = refs[n + 4 :]
    Z, Y, X, H, T = plan.Z, plan.Y, plan.X, plan.H, plan.T
    PB, P0, R, ZB, ZS, YB = plan.PB, plan.P0, plan.hrow, plan.ZB, plan.ZS, plan.YB
    offset = scal[1]
    halves = range(H)
    row = lax.broadcasted_iota(jnp.int32, (8, LANES), 0)
    lane = lax.broadcasted_iota(jnp.int32, (8, LANES), 1)
    first_half = row < 4
    spare = (row == 3) | (row == 7)
    zero = jnp.zeros((8, LANES), f32)

    def shift_left(parts):
        rolled = [pltpu.roll(p, LANES - 1, 1) for p in parts] + [zero]
        return [jnp.where(lane == LANES - 1, rolled[h + 1], rolled[h]) for h in halves]

    def shift_right(parts):
        rolled = [zero] + [pltpu.roll(p, 1, 1) for p in parts]
        return [jnp.where(lane == 0, rolled[h], rolled[h + 1]) for h in halves]

    def columns(parts):
        ahead = shift_left(parts)
        tiles = []
        for h in halves:
            swapped = pltpu.roll(ahead[h], 4, 0)
            even = jnp.where(first_half, parts[h], swapped)
            odd = jnp.where(first_half, swapped, parts[h])
            high0 = even.astype(bf16).astype(f32)
            high1 = odd.astype(bf16).astype(f32)
            tiles.append(
                (
                    jnp.concatenate([high0, even - high0], 0).astype(bf16),
                    jnp.concatenate([high0, high1], 0).astype(bf16),
                    jnp.concatenate([high1, odd - high1], 0).astype(bf16),
                )
            )
        return tiles

    def put_columns(buffers, z, p, parts):
        for h, tiles in enumerate(columns(parts)):
            for j in range(3):
                for b in buffers:
                    KB[b, z, p, 16 * j : 16 * j + 16, h * LANES : (h + 1) * LANES] = tiles[j]

    mid = slice(R, R + 4 * Y)
    for z in range(Z):
        U[offset + z, :, mid, :] = xv[z, :, : 4 * Y, :]
        V[offset + z, :, mid, :] = xv[z, :, 4 * Y :, :]
    for zrecv, (at_u, at_v, lacks) in zip(zrecvs, halo_places(plan, scal)):
        for i in range(T):
            U[at_u + i, :, mid, :] = zrecv[i]
        for i in range(T - 1):
            V[at_v + i, :, mid, :] = zrecv[T + i]
        V[lacks, :, mid, :] = jnp.zeros((H, 4 * Y, LANES), f32)
    U[ZB:, :, :, :] = jnp.zeros((ZS - ZB, H, 4 * YB, LANES), f32)
    V[ZB:, :, :, :] = jnp.zeros((ZS - ZB, H, 4 * YB, LANES), f32)
    for s in range(T):
        G[s] = jnp.zeros((H, 4 * YB, LANES), f32)
        G[s, :, mid, :] = gown[s]
    for s, k, n_pairs, layer, at in g_slots(plan):
        low = R - 8 * n_pairs + 8 * k
        G[s, :, low : low + 8, :] = from_prev[layer, :, at : at + 8, :]
        high = R + 4 * Y + 8 * k
        G[s, :, high : high + 8, :] = from_next[layer, :, at : at + 8, :]

    def begin(z, carry):
        for source, here in ((from_prev, slice(0, R)), (from_next, slice(R + 4 * Y, 4 * YB))):
            U[z, :, here, :] = source[z, :, :R, :]
            V[z, :, here, :] = source[z, :, R:, :]
        return carry

    lax.fori_loop(0, ZB, begin, 0)

    n_levels = tables.shape[1]

    def prepare(z, carry):
        for h in halves:
            for y in range(0, plan.YL, 8):
                count = min(8, YB - y)
                if count == 8:
                    level = U[z, h, pl.ds(4 * y + 3, 8, stride=4), :]
                    first = y
                else:
                    first = YB - 8
                    level = U[z, h, pl.ds(4 * first + 3, 8, stride=4), :]
                dil = jnp.zeros((8, LANES), f32)
                she = jnp.zeros((8, LANES), f32)
                for k in range(n_levels):
                    here = level == float(k + 1)
                    dil = jnp.where(here, tables[0, k], dil)
                    she = jnp.where(here, tables[1, k], she)
                lam[z, h, first : first + 8, :] = dil
                mu[z, h, first : first + 8, :] = she
        for p in range(PB):
            at = slice(8 * p, 8 * p + 8)
            for h in halves:
                v = V[z, h, at, :]
                mass = jnp.where(
                    first_half,
                    jnp.broadcast_to(v[3:4, :], (8, LANES)),
                    jnp.broadcast_to(v[7:8, :], (8, LANES)),
                )
                DM[z, h, at, :] = jnp.where(spare, 0.0, time_step * mass)
            put_columns((0, 1), z, p, [U[z, h, at, :] for h in halves])
        for b in range(2):
            KB[b, z, PB] = jnp.zeros((48, X), bf16)
        return carry

    lax.fori_loop(0, ZS, prepare, 0)

    bottom = offset + Z - 1
    wave = jnp.zeros((8, LANES), f32)
    for c in range(3):
        wave = jnp.where((row == c) | (row == 4 + c), imp[c], wave)
    wave = jnp.where(scal[2] == 1, wave, zero)
    for h in halves:
        for p in range(PB):
            at = slice(8 * p, 8 * p + 8)
            CI[h, at, :] = wave * DM[bottom, h, at, :]

    def one_step(s, final):
        d = T - 1 - s
        cur, new = s % 2, 1 - s % 2
        p_first = (plan.hy - d - 1) // 2
        p_last = (plan.hy + Y - 1 + d) // 2
        if plan.D == 1:
            p_z0, count = 0, -(-Z // 2)
        elif plan.swap:
            top = scal[0] == 0
            n_low = -(-(Z + d + 1) // 2)
            count = jnp.where(top, -(-(Z + d) // 2), n_low)
            p_z0 = jnp.where(top, 0, ZB - 2 * n_low)
        else:
            p_z0 = T - d - 1
            count = -(-(Z + 2 * d + 1) // 2)

        for p in range(p_first, p_last + 1):
            at = slice(8 * p, 8 * p + 8)
            for h in halves:
                v = V[bottom, h, at, :]
                V[bottom, h, at, :] = v + CI[h, at, :] * (G[s, h, at, :] - v)
        for p in range(p_first, p_last + 1):
            F[p] = jnp.zeros((2, H, 8, LANES), f32)

        def finish(z, p, g0, g1):
            at = slice(8 * p, 8 * p + 8)
            other = [
                pltpu.roll(jnp.where(first_half, g1[h], g0[h]), 4, 0) for h in halves
            ]
            other = shift_right(other)
            fresh = []
            for h in halves:
                force = jnp.where(first_half, g0[h], g1[h]) + other[h]
                v = V[z, h, at, :] - DM[z, h, at, :] * force
                u = U[z, h, at, :] + time_step * v
                V[z, h, at, :] = v
                U[z, h, at, :] = u
                fresh.append(u)
            if not final:
                put_columns((new,), z, p, fresh)

        def two_layers(i, carry):
            z0 = p_z0 + 2 * i
            side = [[zero for _ in halves] for _ in range(3)]
            for p in range(p_first, p_last + 1):
                right = jnp.concatenate(
                    [
                        KB[cur, z0, p],
                        KB[cur, z0, p + 1, :32],
                        KB[cur, z0 + 1, p],
                        KB[cur, z0 + 1, p + 1, :32],
                        KB[cur, z0 + 2, p],
                        KB[cur, z0 + 2, p + 1],
                    ],
                    0,
                )
                product = jnp.dot(weights[...], right, preferred_element_type=f32)
                node = [[None] * 3 for _ in range(3)]
                for zn in range(3):
                    node[zn][0] = side[zn]
                for y in range(2):
                    above = [F[p, y, h] for h in halves]
                    node[0][y] = above if y else [a + b for a, b in zip(node[0][0], above)]
                for ez in range(2):
                    for ey in range(2):
                        base = 64 * (2 * ez + ey)
                        y = 2 * p + ey
                        for h in halves:
                            lanes = slice(h * LANES, (h + 1) * LANES)
                            dil = jnp.broadcast_to(lam[z0 + ez, h, y : y + 1, :], (8, LANES))
                            she = jnp.broadcast_to(mu[z0 + ez, h, y : y + 1, :], (8, LANES))
                            for dz in range(2):
                                for dy in range(2):
                                    r = base + 8 * (2 * dz + dy)
                                    part = (
                                        dil * product[r : r + 8, lanes]
                                        + she * product[r + 32 : r + 40, lanes]
                                    )
                                    slot = node[ez + dz][ey + dy]
                                    if slot is None:
                                        slot = node[ez + dz][ey + dy] = [None] * H
                                    elif slot is side[ez + dz]:
                                        slot = node[ez + dz][ey + dy] = list(slot)
                                    slot[h] = part if slot[h] is None else slot[h] + part
                for y in range(2):
                    for h in halves:
                        F[p, y, h] = node[2][y][h]
                finish(z0, p, node[0][0], node[0][1])
                finish(z0 + 1, p, node[1][0], node[1][1])
                side = [node[zn][2] for zn in range(3)]
            return carry

        lax.fori_loop(0, count, two_layers, 0)

    for s in range(T):
        one_step(s, s == T - 1)

    for z in range(Z):
        for h in halves:
            lanes = slice(h * LANES, (h + 1) * LANES)
            for y in range(0, Y, 8):
                for c in range(3):
                    at = pl.ds(R + 4 * y + c, 8, stride=4)
                    out_u[c, z, y : y + 8, lanes] = U[offset + z, h, at, :]
                    out_v[c, z, y : y + 8, lanes] = V[offset + z, h, at, :]


def smem():
    return pl.BlockSpec(memory_space=pltpu.SMEM)


def vmem():
    return pl.BlockSpec(memory_space=pltpu.VMEM)


def per_device(plan, u, v, m, mat, dilation_table, shear_table, stiffness_pair, impedance, mask, inc):
    Z, Y, X, H, T, D, L = plan.Z, plan.Y, plan.X, plan.H, plan.T, plan.D, plan.L
    depth = lax.axis_index("depth")
    scal = jnp.stack(
        [depth, jnp.asarray(plan.offset(depth)), (depth == D - 1).astype(jnp.int32)]
    ).astype(jnp.int32)
    shape = lambda *dims: jax.ShapeDtypeStruct(dims, f32)

    rows, cols = selectors()
    weights = pl.pallas_call(
        matrix_kernel,
        out_shape=jax.ShapeDtypeStruct((256, 256), bf16),
        name="matrix",
    )(stiffness_pair.reshape(48, 24), jnp.asarray(rows, bf16), jnp.asarray(cols, bf16))

    n_sends = 0 if D == 1 else 1 if plan.swap else 2
    packed = pl.pallas_call(
        lambda *refs: pack_kernel(plan, *refs),
        out_shape=[shape(Z, H, 8 * Y, LANES), shape(T, H, 4 * Y, LANES)]
        + [shape(2 * T - 1, H, 4 * Y, LANES)] * n_sends,
        in_specs=[smem()] + [vmem()] * 6,
        out_specs=[vmem()] * (2 + n_sends),
        name="pack",
    )(scal, u, v, m, mat, mask, inc)
    xv, g, sends = packed[0], packed[1], packed[2:]
    if D == 1:
        zrecvs = []
    elif plan.swap:
        zrecvs = [lax.ppermute(sends[0], "depth", [(0, 1), (1, 0)])]
    else:
        zrecvs = [
            lax.ppermute(sends[0], "depth", [(i, i + 1) for i in range(D - 1)]),
            lax.ppermute(sends[1], "depth", [(i + 1, i) for i in range(D - 1)]),
        ]
    edge = shape(plan.ZB + plan.GL, H, 2 * plan.hrow, LANES)
    to_prev, to_next = pl.pallas_call(
        lambda *refs: edge_kernel(plan, *refs),
        out_shape=[edge, edge],
        in_specs=[smem()] + [vmem()] * (2 + len(zrecvs)),
        out_specs=[vmem()] * 2,
        name="edge",
    )(scal, xv, g, *zrecvs)
    from_next = lax.ppermute(to_prev, "lat", [(i + 1, i) for i in range(L - 1)])
    from_prev = lax.ppermute(to_next, "lat", [(i, i + 1) for i in range(L - 1)])
    tables = jnp.stack([dilation_table, shear_table])
    grid = (plan.ZS, H, 4 * plan.YB, LANES)
    new_u, new_v = pl.pallas_call(
        lambda *refs: main_kernel(plan, *refs),
        out_shape=[shape(3, Z, Y, X)] * 2,
        in_specs=[smem()] * 3 + [vmem()] * (5 + len(zrecvs)),
        out_specs=[vmem()] * 2,
        scratch_shapes=[
            pltpu.VMEM(grid, f32),
            pltpu.VMEM(grid, f32),
            pltpu.VMEM(grid, f32),
            pltpu.VMEM((plan.ZS, H, plan.YL, LANES), f32),
            pltpu.VMEM((plan.ZS, H, plan.YL, LANES), f32),
            pltpu.VMEM((T, H, 4 * plan.YB, LANES), f32),
            pltpu.VMEM((H, 4 * plan.YB, LANES), f32),
            pltpu.VMEM((plan.PB, 2, H, 8, LANES), f32),
            pltpu.VMEM((2, plan.ZS, plan.PB + 1, 48, X), bf16),
        ],
        name="steps",
    )(scal, tables, impedance, weights, xv, g, *zrecvs, from_prev, from_next)
    return new_u, new_v


def solution(mesh):
    field = P(None, "depth", "lat", None)
    in_specs = (
        field,
        field,
        P("depth", "lat", None),
        P("depth", "lat", None),
        P(),
        P(),
        P(),
        P(),
        P("lat", None),
        P(None, None, "lat", None),
    )

    def whole(displacement, *rest):
        plan = Plan(mesh, displacement, rest[-1])
        return jax.shard_map(
            lambda *args: per_device(plan, *args),
            mesh=mesh,
            in_specs=in_specs,
            out_specs=(field, field),
            check_vma=False,
        )(displacement, *rest)

    return whole
```

profile of v0, /device:TPU:27, one launch (start us, length us, event | category | flops | bytes accessed | tf_op | source)
XLA Modules:
  0.0 66.5 jit_solution(4208643054887592858)
XLA Ops:
  0.6 0.6 pad_add_fusion.refs_0_
  1.2 2.2 %pack.1 = (f32[8,2,64,128]{3,2,1,0:T(8,128)}, f32[6,2,32,128]{3,2,1,0:T(8,128)}, f32[11,2,32,128]{3,2,1,0:T(8,128)}) custom-call(s32[3]{0:T(128)} %pad_add_fusion.refs_0_, f32[3,8,8,256]{3,2,1,0:T(8,128)} %refs_1_.1, f32[3,8,8,256]{3,2,1,0:T(8,128)} %refs_2_.2, f32[8,8,256]{2,1,0:T(8,128)} %refs_3_.1, s32[8,8,256]{2,1,0:T(8,128)} %refs_4_.1, ...), custom_call_target="tpu_custom_call" | custom-call | tf_op jit(solution)/shard_map/pack/pallas_call | solution.py:424
  3.4 0.3 collective-permute-start
  3.7 9.3 %collective-permute-done.refs_3_.refs_6_ = f32[11,2,32,128]{3,2,1,0:T(8,128)S(1)} collective-permute-done((f32[11,2,32,128]{3,2,1,0:T(8,128)}, f32[11,2,32,128]{3,2,1,0:T(8,128)S(1)}, u32[]{:S(2)}, u32[]{:S(2)}) %collective-permute-start) | collective-permute-done | bytes 360480 | tf_op jit(solution)/shard_map/ppermute | solution.py:436
  13.0 0.0 copy-start
  13.0 0.7 %copy-done = f32[11,2,32,128]{3,2,1,0:T(8,128)} copy-done((f32[11,2,32,128]{3,2,1,0:T(8,128)}, f32[11,2,32,128]{3,2,1,0:T(8,128)S(1)}, u32[]{:S(2)}) %copy-start) | copy-done | bytes 360472
  13.7 2.5 %edge.1 = (f32[16,2,48,128]{3,2,1,0:T(8,128)}, f32[16,2,48,128]{3,2,1,0:T(8,128)}) custom-call(s32[3]{0:T(128)} %pad_add_fusion.refs_0_, f32[8,2,64,128]{3,2,1,0:T(8,128)} %get-tuple-element.7.refs_1_.refs_4_, f32[6,2,32,128]{3,2,1,0:T(8,128)} %get-tuple-element.8.refs_2_.refs_5_, f32[11,2,32,128]{3,2,1,0:T(8,128)} %copy-done), custom_call_target="tpu_custom_call" | custom-call | tf_op jit(solution)/shard_map/edge/pallas_call | solution.py:443
  16.2 4.6 %collective-permute-start.1 = (f32[16,2,48,128]{3,2,1,0:T(8,128)}, f32[16,2,48,128]{3,2,1,0:T(8,128)S(1)}, u32[]{:S(2)}, u32[]{:S(2)}) collective-permute-start(f32[16,2,48,128]{3,2,1,0:T(8,128)} %get-tuple-element.10), channel_id=1, source_target_pairs={{0,1},{1,2},{2,3},{3,4},{4,5},{5,6},{6,7},{7,8},{8,9},{9,10},{10,1... | collective-permute-start | bytes 2359304 | tf_op jit(solution)/shard_map/ppermute | solution.py:451
  20.7 1.9 %collective-permute-start.2 = (f32[16,2,48,128]{3,2,1,0:T(8,128)}, f32[16,2,48,128]{3,2,1,0:T(8,128)S(1)}, u32[]{:S(2)}, u32[]{:S(2)}) collective-permute-start(f32[16,2,48,128]{3,2,1,0:T(8,128)} %get-tuple-element.11), channel_id=1, source_target_pairs={{1,0},{2,1},{3,2},{4,3},{5,4},{6,5},{7,6},{8,7},{9,8},{10,9},{11,1... | collective-permute-start | bytes 2359304 | tf_op jit(solution)/shard_map/ppermute | solution.py:450
  22.7 2.1 %matrix.1.refs_3_ = bf16[256,256]{1,0:T(8,128)(2,1)} custom-call(f32[48,24]{1,0:T(8,128)} %bitcast.6, bf16[4,64,48]{2,1,0:T(8,128)(2,1)} %constant.14.clone.rows_ref, bf16[2,4,24,256]{3,2,1,0:T(8,128)(2,1)} %constant.15.clone.cols_ref), custom_call_target="tpu_custom_call" | custom-call | tf_op jit(solution)/shard_map/matrix/pallas_call | solution.py:417
  24.7 0.0 copy-start.3
  24.7 0.0 copy-start.4
  24.7 0.7 copy-done.3
  25.4 0.0 copy-done.4
  25.4 0.5 pad_maximum_fusion.refs_1_
  25.9 4.0 %collective-permute-done.1.refs_7_ = f32[16,2,48,128]{3,2,1,0:T(8,128)S(1)} collective-permute-done((f32[16,2,48,128]{3,2,1,0:T(8,128)}, f32[16,2,48,128]{3,2,1,0:T(8,128)S(1)}, u32[]{:S(2)}, u32[]{:S(2)}) %collective-permute-start.1) | collective-permute-done | bytes 786464 | tf_op jit(solution)/shard_map/ppermute | solution.py:451
  30.0 0.0 copy-start.1
  30.0 9.9 %collective-permute-done.2.refs_8_ = f32[16,2,48,128]{3,2,1,0:T(8,128)S(1)} collective-permute-done((f32[16,2,48,128]{3,2,1,0:T(8,128)}, f32[16,2,48,128]{3,2,1,0:T(8,128)S(1)}, u32[]{:S(2)}, u32[]{:S(2)}) %collective-permute-start.2) | collective-permute-done | bytes 786464 | tf_op jit(solution)/shard_map/ppermute | solution.py:450
  39.9 0.0 copy-done.1
  39.9 0.0 copy-start.2
  39.9 0.9 %copy-done.2 = f32[16,2,48,128]{3,2,1,0:T(8,128)} copy-done((f32[16,2,48,128]{3,2,1,0:T(8,128)}, f32[16,2,48,128]{3,2,1,0:T(8,128)S(1)}, u32[]{:S(2)}) %copy-start.2) | copy-done | bytes 786456
  40.8 25.8 %steps.1 = (f32[3,8,8,256]{3,2,1,0:T(8,128)}, f32[3,8,8,256]{3,2,1,0:T(8,128)}) custom-call(s32[3]{0:T(128)} %pad_add_fusion.refs_0_, f32[2,8]{1,0:T(2,128)} %pad_maximum_fusion.refs_1_, f32[3]{0:T(128)} %refs_2_.3, bf16[256,256]{1,0:T(8,128)(2,1)} %matrix.1.refs_3_, f32[8,2,64,128]{3,2,1,0:T(8,128)} %get-tuple-element.7.refs_1_.refs_4_, ...), custom_call_target="tpu_custom_call" | custom-call | tf_op jit(solution)/shard_map/steps/pallas_call | solution.py:454
Async XLA Ops:
  3.4 9.5 %collective-permute-start = (f32[11,2,32,128]{3,2,1,0:T(8,128)}, f32[11,2,32,128]{3,2,1,0:T(8,128)S(1)}, u32[]{:S(2)}, u32[]{:S(2)}) collective-permute-start(f32[11,2,32,128]{3,2,1,0:T(8,128)} %get-tuple-element.9), channel_id=1, source_target_pairs={{0,16},{16,0},{1,17},{17,1},{2,18},{18,2},{3,19},{19,3},{4,20},{20... | collective-permute-start | bytes 1081352 | tf_op jit(solution)/shard_map/ppermute | solution.py:436
  13.0 0.7 %copy-start = (f32[11,2,32,128]{3,2,1,0:T(8,128)}, f32[11,2,32,128]{3,2,1,0:T(8,128)S(1)}, u32[]{:S(2)}) copy-start(f32[11,2,32,128]{3,2,1,0:T(8,128)S(1)} %collective-permute-done.refs_3_.refs_6_) | copy-start | bytes 1081348
  16.2 13.8 %collective-permute-start.1 = (f32[16,2,48,128]{3,2,1,0:T(8,128)}, f32[16,2,48,128]{3,2,1,0:T(8,128)S(1)}, u32[]{:S(2)}, u32[]{:S(2)}) collective-permute-start(f32[16,2,48,128]{3,2,1,0:T(8,128)} %get-tuple-element.10), channel_id=1, source_target_pairs={{0,1},{1,2},{2,3},{3,4},{4,5},{5,6},{6,7},{7,8},{8,9},{9,10},{10,1... | collective-permute-start | bytes 2359304 | tf_op jit(solution)/shard_map/ppermute | solution.py:451
  20.7 19.1 %collective-permute-start.2 = (f32[16,2,48,128]{3,2,1,0:T(8,128)}, f32[16,2,48,128]{3,2,1,0:T(8,128)S(1)}, u32[]{:S(2)}, u32[]{:S(2)}) collective-permute-start(f32[16,2,48,128]{3,2,1,0:T(8,128)} %get-tuple-element.11), channel_id=1, source_target_pairs={{1,0},{2,1},{3,2},{4,3},{5,4},{6,5},{7,6},{8,7},{9,8},{10,9},{11,1... | collective-permute-start | bytes 2359304 | tf_op jit(solution)/shard_map/ppermute | solution.py:450
  24.7 0.7 copy-start.3
  24.7 0.7 %copy-start.4 = (f32[8]{0:T(128)S(1)}, f32[8]{0:T(128)}, u32[]{:S(2)}) copy-start(f32[8]{0:T(128)} %param.16) | copy-start | bytes 100
  30.0 9.9 %copy-start.1 = (f32[16,2,48,128]{3,2,1,0:T(8,128)}, f32[16,2,48,128]{3,2,1,0:T(8,128)S(1)}, u32[]{:S(2)}) copy-start(f32[16,2,48,128]{3,2,1,0:T(8,128)S(1)} %collective-permute-done.1.refs_7_) | copy-start | bytes 2359300
  39.9 0.9 %copy-start.2 = (f32[16,2,48,128]{3,2,1,0:T(8,128)}, f32[16,2,48,128]{3,2,1,0:T(8,128)S(1)}, u32[]{:S(2)}) copy-start(f32[16,2,48,128]{3,2,1,0:T(8,128)S(1)} %collective-permute-done.2.refs_8_) | copy-start | bytes 2359300
where the time goes:
time: 66.8 us; the launch traced here: 66.5 us
  Pallas kernels  32.5 us (49%)
  waiting for transfers between devices  23.2 us (35%)
  starting transfers between devices  6.73 us (10%)
  local copies, waits for them, and re-layouts  2.32 us (3%)
  other arithmetic  1.15 us (2%)
    pallas_call x1, Pallas kernels, per_device(): pl.pallas_call(lambda *refs: main_kernel(plan, *refs), out_shape=[shape(3...  25.8 us
    ppermute x1, waiting for transfers between devices, per_device(): from_next = lax.ppermute(to_prev, 'lat', [(i + 1, i) for i in range(L - 1)])  9.88 us
    ppermute x1, waiting for transfers between devices, per_device(): zrecvs = [lax.ppermute(sends[0], 'depth', [(0, 1), (1, 0)])]  9.25 us
    ppermute x1, starting transfers between devices, per_device(): from_prev = lax.ppermute(to_next, 'lat', [(i, i + 1) for i in range(L - 1)])  4.55 us
    ppermute x1, waiting for transfers between devices, per_device(): from_prev = lax.ppermute(to_next, 'lat', [(i, i + 1) for i in range(L - 1)])  4.02 us
    pallas_call x1, Pallas kernels, per_device(): pl.pallas_call(lambda *refs: edge_kernel(plan, *refs), out_shape=[edge, e...  2.49 us
    unnamed x10, local copies, waits for them, and re-layouts  2.32 us
    pallas_call x1, Pallas kernels, per_device(): pl.pallas_call(lambda *refs: pack_kernel(plan, *refs), out_shape=[shape(Z...  2.19 us
  transfers between devices with their start and end apart: 3, of which 3 were waited for; matrix products, arithmetic and copies ran while one was open for 1% of the time, Pallas kernels for 3%

commit v1 on v0

--- a/solution.py
+++ b/solution.py
@@ -33,23 +33,27 @@
         self.ZS = self.ZB + 2
         self.YL = -(-self.YB // 8) * 8
         self.gpairs = [-(-(T - 1 - s) // 2) for s in range(T)]
-        self.grows = 8 * sum(self.gpairs)
         self.hrow = 4 * self.hy
-        self.GL = -(-self.grows // (2 * self.hrow))
 
     def offset(self, depth):
         if self.D == 1:
             return 0
         return depth * self.T if self.swap else self.T
 
-
-def g_slots(plan):
-    slots, g = [], 0
-    for s, n in enumerate(plan.gpairs):
-        for k in range(n):
-            slots.append((s, k, n, plan.ZB + (8 * g) // (2 * plan.hrow), (8 * g) % (2 * plan.hrow)))
-            g += 1
-    return slots
+    def own_tiles(self):
+        n = self.hy // 2
+        tiles = [(f, z, h, p) for f in (0, 1) for z in range(self.Z) for h in range(self.H) for p in range(n)]
+        waves = [
+            (s, h, k, n_pairs)
+            for s, n_pairs in enumerate(self.gpairs)
+            for h in range(self.H)
+            for k in range(n_pairs)
+        ]
+        return tiles, waves
+
+    def corner_tiles(self):
+        n = self.hy // 2
+        return [(i, h, p) for i in range(2 * self.T - 1) for h in range(self.H) for p in range(n)]
 
 
 def selectors():
@@ -95,7 +99,7 @@
         out_ref[64 * e : 64 * e + 64, :] = total.astype(bf16)
 
 
-def pack_kernel(plan, scal, u, v, m, mat, mask, inc, xv, g, *zsends):
+def pack_kernel(plan, scal, u, v, m, mat, mask, inc, xv, g, to_prev, to_next, *zsends):
     Z, Y, H, T = plan.Z, plan.Y, plan.H, plan.T
     for z in range(Z):
         for h in range(H):
@@ -116,6 +120,14 @@
                 for c in range(3):
                     g[s, h, pl.ds(4 * y + c, 8, stride=4), :] = double * inc[s, c, rows, lanes]
                 g[s, h, pl.ds(4 * y + 3, 8, stride=4), :] = jnp.zeros((8, LANES), f32)
+    tiles, waves = plan.own_tiles()
+    for out, low in ((to_prev, 0), (to_next, 4 * Y - plan.hrow)):
+        for t, (f, z, h, p) in enumerate(tiles):
+            at = 4 * Y * f + low + 8 * p
+            out[t] = xv[z, h, at : at + 8, :]
+        for t, (s, h, k, n_pairs) in enumerate(waves):
+            at = 8 * k if low == 0 else 4 * Y - 8 * n_pairs + 8 * k
+            out[len(tiles) + t] = g[s, h, at : at + 8, :]
     for k, zsend in enumerate(zsends):
         if plan.swap:
             first = jnp.where(scal[0] == 0, Z - T, 0)
@@ -144,34 +156,24 @@
     return [(0, 1, 0), (last, last, last + plan.T - 1)]
 
 
-def edge_kernel(plan, scal, xv, g, *refs):
+def corner_kernel(plan, *refs):
     n = len(refs) - 2
-    zrecvs, to_prev, to_next = refs[:n], refs[n], refs[n + 1]
-    Y, T, R = plan.Y, plan.T, plan.hrow
-    offset = scal[1]
-    sides = ((to_prev, 0), (to_next, 4 * Y - R))
-    for z in range(plan.Z):
-        for out, row in sides:
-            out[offset + z, :, :R, :] = xv[z, :, row : row + R, :]
-            out[offset + z, :, R:, :] = xv[z, :, 4 * Y + row : 4 * Y + row + R, :]
-    for zrecv, (at_u, at_v, lacks) in zip(zrecvs, halo_places(plan, scal)):
-        for out, row in sides:
-            for i in range(T):
-                out[at_u + i, :, :R, :] = zrecv[i, :, row : row + R, :]
-            for i in range(T - 1):
-                out[at_v + i, :, R:, :] = zrecv[T + i, :, row : row + R, :]
-            out[lacks, :, R:, :] = jnp.zeros((plan.H, R, LANES), f32)
-    for s, k, n_pairs, layer, row in g_slots(plan):
-        to_prev[layer, :, row : row + 8, :] = g[s, :, 8 * k : 8 * k + 8, :]
-        at = 4 * Y - 8 * n_pairs + 8 * k
-        to_next[layer, :, row : row + 8, :] = g[s, :, at : at + 8, :]
+    zrecvs, (to_prev, to_next) = refs[:n], refs[n:]
+    tiles = plan.corner_tiles()
+    for k, zrecv in enumerate(zrecvs):
+        for t, (i, h, p) in enumerate(tiles):
+            t += k * len(tiles)
+            to_prev[t] = zrecv[i, h, 8 * p : 8 * p + 8, :]
+            low = 4 * plan.Y - plan.hrow + 8 * p
+            to_next[t] = zrecv[i, h, low : low + 8, :]
 
 
 def main_kernel(plan, scal, tables, imp, weights, xv, gown, *refs):
-    n = len(refs) - 2 - 2 - 9
-    zrecvs = refs[:n]
-    from_prev, from_next, out_u, out_v = refs[n : n + 4]
-    U, V, DM, lam, mu, G, CI, F, KB = refs[n + 4 :]
+    n = 0 if plan.D == 1 else 1 if plan.swap else 2
+    zrecvs, from_prev, from_next = refs[:n], refs[n], refs[n + 1]
+    corners = refs[n + 2 : len(refs) - 11]
+    out_u, out_v = refs[len(refs) - 11 : len(refs) - 9]
+    U, V, DM, lam, mu, G, CI, F, KB = refs[len(refs) - 9 :]
     Z, Y, X, H, T = plan.Z, plan.Y, plan.X, plan.H, plan.T
     PB, P0, R, ZB, ZS, YB = plan.PB, plan.P0, plan.hrow, plan.ZB, plan.ZS, plan.YB
     offset = scal[1]
@@ -229,19 +231,23 @@
     for s in range(T):
         G[s] = jnp.zeros((H, 4 * YB, LANES), f32)
         G[s, :, mid, :] = gown[s]
-    for s, k, n_pairs, layer, at in g_slots(plan):
-        low = R - 8 * n_pairs + 8 * k
-        G[s, :, low : low + 8, :] = from_prev[layer, :, at : at + 8, :]
-        high = R + 4 * Y + 8 * k
-        G[s, :, high : high + 8, :] = from_next[layer, :, at : at + 8, :]
-
-    def begin(z, carry):
-        for source, here in ((from_prev, slice(0, R)), (from_next, slice(R + 4 * Y, 4 * YB))):
-            U[z, :, here, :] = source[z, :, :R, :]
-            V[z, :, here, :] = source[z, :, R:, :]
-        return carry
-
-    lax.fori_loop(0, ZB, begin, 0)
+    own, waves = plan.own_tiles()
+    for source, low in ((from_prev, 0), (from_next, R + 4 * Y)):
+        for t, (f, z, h, p) in enumerate(own):
+            (V if f else U)[offset + z, h, low + 8 * p : low + 8 * p + 8, :] = source[t]
+        for t, (s, h, k, n_pairs) in enumerate(waves):
+            at = (R - 8 * n_pairs if low == 0 else low) + 8 * k
+            G[s, h, at : at + 8, :] = source[len(own) + t]
+    tiles = plan.corner_tiles()
+    for k, (at_u, at_v, lacks) in enumerate(halo_places(plan, scal)):
+        for source, low in zip(corners, (0, R + 4 * Y)):
+            for t, (i, h, p) in enumerate(tiles):
+                at = slice(low + 8 * p, low + 8 * p + 8)
+                if i < T:
+                    U[at_u + i, h, at, :] = source[k * len(tiles) + t]
+                else:
+                    V[at_v + i - T, h, at, :] = source[k * len(tiles) + t]
+            V[lacks, :, low : low + R, :] = jnp.zeros((H, R, LANES), f32)
 
     n_levels = tables.shape[1]
 
@@ -299,9 +305,8 @@
             p_z0, count = 0, -(-Z // 2)
         elif plan.swap:
             top = scal[0] == 0
-            n_low = -(-(Z + d + 1) // 2)
-            count = jnp.where(top, -(-(Z + d) // 2), n_low)
-            p_z0 = jnp.where(top, 0, ZB - 2 * n_low)
+            count = -(-(Z + d + 1) // 2)
+            p_z0 = jnp.where(top, 0, ZB - 2 * count)
         else:
             p_z0 = T - d - 1
             count = -(-(Z + 2 * d + 1) // 2)
@@ -382,7 +387,16 @@
                 side = [node[zn][2] for zn in range(3)]
             return carry
 
-        lax.fori_loop(0, count, two_layers, 0)
+        def chunk(first, rows):
+            for i in range(rows):
+                two_layers(first + i, 0)
+
+        U3 = 3
+        full, rest = count // U3, count % U3
+        if full:
+            lax.fori_loop(0, full * scal[3], lambda i, c: (chunk(U3 * i, U3), c)[1], 0)
+        if rest:
+            lax.fori_loop(0, scal[3], lambda i, c: (chunk(U3 * full, rest), c)[1], 0)
 
     for s in range(T):
         one_step(s, s == T - 1)
@@ -409,7 +423,7 @@
     Z, Y, X, H, T, D, L = plan.Z, plan.Y, plan.X, plan.H, plan.T, plan.D, plan.L
     depth = lax.axis_index("depth")
     scal = jnp.stack(
-        [depth, jnp.asarray(plan.offset(depth)), (depth == D - 1).astype(jnp.int32)]
+        [depth, jnp.asarray(plan.offset(depth)), (depth == D - 1).astype(jnp.int32), jnp.asarray(1)]
     ).astype(jnp.int32)
     shape = lambda *dims: jax.ShapeDtypeStruct(dims, f32)
 
@@ -421,15 +435,20 @@
     )(stiffness_pair.reshape(48, 24), jnp.asarray(rows, bf16), jnp.asarray(cols, bf16))
 
     n_sends = 0 if D == 1 else 1 if plan.swap else 2
+    tiles, waves = plan.own_tiles()
+    edge = shape(len(tiles) + len(waves), 8, LANES)
     packed = pl.pallas_call(
         lambda *refs: pack_kernel(plan, *refs),
-        out_shape=[shape(Z, H, 8 * Y, LANES), shape(T, H, 4 * Y, LANES)]
+        out_shape=[shape(Z, H, 8 * Y, LANES), shape(T, H, 4 * Y, LANES), edge, edge]
         + [shape(2 * T - 1, H, 4 * Y, LANES)] * n_sends,
         in_specs=[smem()] + [vmem()] * 6,
-        out_specs=[vmem()] * (2 + n_sends),
+        out_specs=[vmem()] * (4 + n_sends),
         name="pack",
     )(scal, u, v, m, mat, mask, inc)
-    xv, g, sends = packed[0], packed[1], packed[2:]
+    xv, g, to_prev, to_next = packed[:4]
+    sends = packed[4:]
+    up = [(i + 1, i) for i in range(L - 1)]
+    down = [(i, i + 1) for i in range(L - 1)]
     if D == 1:
         zrecvs = []
     elif plan.swap:
@@ -439,22 +458,25 @@
             lax.ppermute(sends[0], "depth", [(i, i + 1) for i in range(D - 1)]),
             lax.ppermute(sends[1], "depth", [(i + 1, i) for i in range(D - 1)]),
         ]
-    edge = shape(plan.ZB + plan.GL, H, 2 * plan.hrow, LANES)
-    to_prev, to_next = pl.pallas_call(
-        lambda *refs: edge_kernel(plan, *refs),
-        out_shape=[edge, edge],
-        in_specs=[smem()] + [vmem()] * (2 + len(zrecvs)),
-        out_specs=[vmem()] * 2,
-        name="edge",
-    )(scal, xv, g, *zrecvs)
-    from_next = lax.ppermute(to_prev, "lat", [(i + 1, i) for i in range(L - 1)])
-    from_prev = lax.ppermute(to_next, "lat", [(i, i + 1) for i in range(L - 1)])
+    from_next = lax.ppermute(to_prev, "lat", up)
+    from_prev = lax.ppermute(to_next, "lat", down)
+    corners = []
+    if zrecvs:
+        corner = shape(len(zrecvs) * len(plan.corner_tiles()), 8, LANES)
+        corner_prev, corner_next = pl.pallas_call(
+            lambda *refs: corner_kernel(plan, *refs),
+            out_shape=[corner, corner],
+            in_specs=[vmem()] * len(zrecvs),
+            out_specs=[vmem()] * 2,
+            name="corner",
+        )(*zrecvs)
+        corners = [lax.ppermute(corner_next, "lat", down), lax.ppermute(corner_prev, "lat", up)]
     tables = jnp.stack([dilation_table, shear_table])
     grid = (plan.ZS, H, 4 * plan.YB, LANES)
     new_u, new_v = pl.pallas_call(
         lambda *refs: main_kernel(plan, *refs),
         out_shape=[shape(3, Z, Y, X)] * 2,
-        in_specs=[smem()] * 3 + [vmem()] * (5 + len(zrecvs)),
+        in_specs=[smem()] * 3 + [vmem()] * (5 + len(zrecvs) + len(corners)),
         out_specs=[vmem()] * 2,
         scratch_shapes=[
             pltpu.VMEM(grid, f32),
@@ -468,7 +490,7 @@
             pltpu.VMEM((2, plan.ZS, plan.PB + 1, 48, X), bf16),
         ],
         name="steps",
-    )(scal, tables, impedance, weights, xv, g, *zrecvs, from_prev, from_next)
+    )(scal, tables, impedance, weights, xv, g, *zrecvs, from_prev, from_next, *corners)
     return new_u, new_v
 
 

time: 66.8 us -> 49.3 us (0.74)
  the two profiles are of different devices: /device:TPU:27 before, /device:TPU:1 now
where the time goes in v1:
time: 49.3 us; the launch traced here: 48.9 us
  Pallas kernels  25.4 us (52%)
  starting transfers between devices  14.4 us (29%)
  waiting for transfers between devices  5.16 us (10%)
  local copies, waits for them, and re-layouts  2.12 us (4%)
  other arithmetic  1.15 us (2%)
  between operations  0.71 us (1%)
    pallas_call x1, Pallas kernels, per_device(): pl.pallas_call(lambda *refs: main_kernel(plan, *refs), out_shape=[shape(3...  18.9 us
    ppermute x1, starting transfers between devices, per_device(): lax.ppermute(corner_next, 'lat', down)  4.52 us
    ppermute x1, starting transfers between devices, per_device(): from_prev = lax.ppermute(to_next, 'lat', down)  3.98 us
    ppermute x1, waiting for transfers between devices, per_device(): lax.ppermute(corner_prev, 'lat', up)  2.74 us
    pallas_call x1, Pallas kernels, per_device(): pl.pallas_call(lambda *refs: pack_kernel(plan, *refs), out_shape=[shape(Z...  2.53 us
    ppermute x1, waiting for transfers between devices, per_device(): zrecvs = [lax.ppermute(sends[0], 'depth', [(0, 1), (1, 0)])]  2.41 us
    unnamed x14, local copies, waits for them, and re-layouts  2.12 us
    pallas_call x1, Pallas kernels, per_device(): pl.pallas_call(matrix_kernel, out_shape=jax.ShapeDtypeStruct((256, 256),...  2.07 us
  transfers between devices with their start and end apart: 5, of which 2 were waited for; matrix products, arithmetic and copies ran while one was open for 1% of the time, Pallas kernels for 8%

profile of v1, /device:TPU:1, one launch (start us, length us, event | category | flops | bytes accessed | tf_op | source)
XLA Modules:
  0.0 48.9 jit_solution(14114342025893153368)
XLA Ops:
  0.6 0.6 %pad_add_fusion.refs_0_ = s32[4]{0:T(128)} fusion(s32[1]{0:T(128)} %constant.15.clone.1, s32[1]{0:T(128)} %bitcast.2, s32[1]{0:T(128)} %bitcast.1, s32[1]{0:T(128)} %bitcast), kind=kLoop, calls=%fused_computation.1 | loop fusion | flops 12 | bytes 32 | tf_op jit(solution)/shard_map/stack | solution.py:425
  1.3 2.5 %pack.1 = (f32[8,2,64,128]{3,2,1,0:T(8,128)}, f32[6,2,32,128]{3,2,1,0:T(8,128)}, f32[114,8,128]{2,1,0:T(8,128)}, f32[114,8,128]{2,1,0:T(8,128)}, f32[11,2,32,128]{3,2,1,0:T(8,128)}) custom-call(s32[4]{0:T(128)} %pad_add_fusion.refs_0_, f32[3,8,8,256]{3,2,1,0:T(8,128)} %refs_1_.1, f32[3,8,8,256]{3,2,1,0:T(8,128)} %refs_2_.2, f32[8,8,256]{2,1,0:T(8,128)} %refs_3_.1, ...), custom_call_target="tpu_custom_call" | custom-call | tf_op jit(solution)/shard_map/pack/pallas_call | solution.py:440
  3.8 2.0 %collective-permute-start = (f32[11,2,32,128]{3,2,1,0:T(8,128)}, f32[11,2,32,128]{3,2,1,0:T(8,128)S(1)}, u32[]{:S(2)}, u32[]{:S(2)}) collective-permute-start(f32[11,2,32,128]{3,2,1,0:T(8,128)} %get-tuple-element.11), channel_id=1, source_target_pairs={{0,16},{16,0},{1,17},{17,1},{2,18},{18,2},{3,19},{19,3},{4,20},{20... | collective-permute-start | bytes 1081352 | tf_op jit(solution)/shard_map/ppermute | solution.py:455
  5.8 4.0 %collective-permute-start.1 = (f32[114,8,128]{2,1,0:T(8,128)}, f32[114,8,128]{2,1,0:T(8,128)S(1)}, u32[]{:S(2)}, u32[]{:S(2)}) collective-permute-start(f32[114,8,128]{2,1,0:T(8,128)} %get-tuple-element.12), channel_id=1, source_target_pairs={{0,1},{1,2},{2,3},{3,4},{4,5},{5,6},{6,7},{7,8},{8,9},{9,10},{10,1... | collective-permute-start | bytes 1400840 | tf_op jit(solution)/shard_map/ppermute | solution.py:462
  9.8 1.9 %collective-permute-start.2 = (f32[114,8,128]{2,1,0:T(8,128)}, f32[114,8,128]{2,1,0:T(8,128)S(1)}, u32[]{:S(2)}, u32[]{:S(2)}) collective-permute-start(f32[114,8,128]{2,1,0:T(8,128)} %get-tuple-element.13), channel_id=1, source_target_pairs={{1,0},{2,1},{3,2},{4,3},{5,4},{6,5},{7,6},{8,7},{9,8},{10,9},{11,1... | collective-permute-start | bytes 1400840 | tf_op jit(solution)/shard_map/ppermute | solution.py:461
  11.7 2.4 %collective-permute-done.refs_0_.refs_6_ = f32[11,2,32,128]{3,2,1,0:T(8,128)S(1)} collective-permute-done((f32[11,2,32,128]{3,2,1,0:T(8,128)}, f32[11,2,32,128]{3,2,1,0:T(8,128)S(1)}, u32[]{:S(2)}, u32[]{:S(2)}) %collective-permute-start) | collective-permute-done | bytes 360480 | tf_op jit(solution)/shard_map/ppermute | solution.py:455
  14.1 0.7 %copy-done = f32[11,2,32,128]{3,2,1,0:T(8,128)} copy-done((f32[11,2,32,128]{3,2,1,0:T(8,128)}, f32[11,2,32,128]{3,2,1,0:T(8,128)S(1)}, u32[]{:S(2)}) %copy-start) | copy-done | bytes 360472
  14.9 1.8 %corner.1 = (f32[66,8,128]{2,1,0:T(8,128)}, f32[66,8,128]{2,1,0:T(8,128)}) custom-call(f32[11,2,32,128]{3,2,1,0:T(8,128)} %copy-done), custom_call_target="tpu_custom_call" | custom-call | tf_op jit(solution)/shard_map/corner/pallas_call | solution.py:466
  16.7 4.5 %collective-permute-start.3 = (f32[66,8,128]{2,1,0:T(8,128)}, f32[66,8,128]{2,1,0:T(8,128)S(1)}, u32[]{:S(2)}, u32[]{:S(2)}) collective-permute-start(f32[66,8,128]{2,1,0:T(8,128)} %get-tuple-element.14), channel_id=1, source_target_pairs={{0,1},{1,2},{2,3},{3,4},{4,5},{5,6},{6,7},{7,8},{8,9},{9,10},{10,1... | collective-permute-start | bytes 811016 | tf_op jit(solution)/shard_map/ppermute | solution.py:473
  21.2 1.9 %collective-permute-start.4 = (f32[66,8,128]{2,1,0:T(8,128)}, f32[66,8,128]{2,1,0:T(8,128)S(1)}, u32[]{:S(2)}, u32[]{:S(2)}) collective-permute-start(f32[66,8,128]{2,1,0:T(8,128)} %get-tuple-element.15), channel_id=1, source_target_pairs={{1,0},{2,1},{3,2},{4,3},{5,4},{6,5},{7,6},{8,7},{9,8},{10,9},{11,1... | collective-permute-start | bytes 811016 | tf_op jit(solution)/shard_map/ppermute | solution.py:473
  23.2 2.1 %matrix.1.refs_3_ = bf16[256,256]{1,0:T(8,128)(2,1)} custom-call(f32[48,24]{1,0:T(8,128)} %bitcast.6, bf16[4,64,48]{2,1,0:T(8,128)(2,1)} %constant.16.clone.rows_ref, bf16[2,4,24,256]{3,2,1,0:T(8,128)(2,1)} %constant.17.clone.cols_ref), custom_call_target="tpu_custom_call" | custom-call | tf_op jit(solution)/shard_map/matrix/pallas_call | solution.py:431
  25.2 0.7 %copy-done.5 = f32[8]{0:T(128)S(1)} copy-done((f32[8]{0:T(128)S(1)}, f32[8]{0:T(128)}, u32[]{:S(2)}) %copy-start.5) | copy-done | bytes 56
  25.9 0.0 copy-done.6
  25.9 0.5 %pad_maximum_fusion.refs_1_ = f32[2,8]{1,0:T(2,128)} fusion(f32[1,8]{1,0:T(1,128)S(1)} %bitcast.7, f32[1,8]{1,0:T(1,128)S(1)} %bitcast.8), kind=kLoop, calls=%fused_computation | loop fusion | flops 16 | bytes 128 | tf_op jit(solution)/shard_map/stack | solution.py:474
  26.4 0.0 collective-permute-done.1.refs_7_
  26.4 0.0 collective-permute-done.2.refs_8_
  26.5 0.0 copy-start.2
  26.5 0.0 collective-permute-done.3.refs_9_
  26.5 0.0 copy-start.3
  26.5 2.7 %collective-permute-done.4.refs_10_ = f32[66,8,128]{2,1,0:T(8,128)S(1)} collective-permute-done((f32[66,8,128]{2,1,0:T(8,128)}, f32[66,8,128]{2,1,0:T(8,128)S(1)}, u32[]{:S(2)}, u32[]{:S(2)}) %collective-permute-start.4) | collective-permute-done | bytes 270368 | tf_op jit(solution)/shard_map/ppermute | solution.py:473
  29.2 0.0 copy-done.1
  29.2 0.0 copy-done.3
  29.2 0.7 %copy-done.4 = f32[66,8,128]{2,1,0:T(8,128)} copy-done((f32[66,8,128]{2,1,0:T(8,128)}, f32[66,8,128]{2,1,0:T(8,128)S(1)}, u32[]{:S(2)}) %copy-start.4) | copy-done | bytes 270360
  29.9 18.9 %steps.1 = (f32[3,8,8,256]{3,2,1,0:T(8,128)}, f32[3,8,8,256]{3,2,1,0:T(8,128)}) custom-call(s32[4]{0:T(128)} %pad_add_fusion.refs_0_, f32[2,8]{1,0:T(2,128)} %pad_maximum_fusion.refs_1_, f32[3]{0:T(128)} %refs_2_.3, bf16[256,256]{1,0:T(8,128)(2,1)} %matrix.1.refs_3_, f32[8,2,64,128]{3,2,1,0:T(8,128)} %get-tuple-element.9.refs_4_, ...), custom_call_target="tpu_custom_call" | custom-call | tf_op jit(solution)/shard_map/steps/pallas_call | solution.py:476
  (6 shorter events, 0.0 us)
Async XLA Ops:
  3.8 10.4 %collective-permute-start = (f32[11,2,32,128]{3,2,1,0:T(8,128)}, f32[11,2,32,128]{3,2,1,0:T(8,128)S(1)}, u32[]{:S(2)}, u32[]{:S(2)}) collective-permute-start(f32[11,2,32,128]{3,2,1,0:T(8,128)} %get-tuple-element.11), channel_id=1, source_target_pairs={{0,16},{16,0},{1,17},{17,1},{2,18},{18,2},{3,19},{19,3},{4,20},{20... | collective-permute-start | bytes 1081352 | tf_op jit(solution)/shard_map/ppermute | solution.py:455
  5.8 20.6 %collective-permute-start.1 = (f32[114,8,128]{2,1,0:T(8,128)}, f32[114,8,128]{2,1,0:T(8,128)S(1)}, u32[]{:S(2)}, u32[]{:S(2)}) collective-permute-start(f32[114,8,128]{2,1,0:T(8,128)} %get-tuple-element.12), channel_id=1, source_target_pairs={{0,1},{1,2},{2,3},{3,4},{4,5},{5,6},{6,7},{7,8},{8,9},{9,10},{10,1... | collective-permute-start | bytes 1400840 | tf_op jit(solution)/shard_map/ppermute | solution.py:462
  9.8 16.7 %collective-permute-start.2 = (f32[114,8,128]{2,1,0:T(8,128)}, f32[114,8,128]{2,1,0:T(8,128)S(1)}, u32[]{:S(2)}, u32[]{:S(2)}) collective-permute-start(f32[114,8,128]{2,1,0:T(8,128)} %get-tuple-element.13), channel_id=1, source_target_pairs={{1,0},{2,1},{3,2},{4,3},{5,4},{6,5},{7,6},{8,7},{9,8},{10,9},{11,1... | collective-permute-start | bytes 1400840 | tf_op jit(solution)/shard_map/ppermute | solution.py:461
  14.1 0.7 %copy-start = (f32[11,2,32,128]{3,2,1,0:T(8,128)}, f32[11,2,32,128]{3,2,1,0:T(8,128)S(1)}, u32[]{:S(2)}) copy-start(f32[11,2,32,128]{3,2,1,0:T(8,128)S(1)} %collective-permute-done.refs_0_.refs_6_) | copy-start | bytes 1081348
  16.7 9.8 %collective-permute-start.3 = (f32[66,8,128]{2,1,0:T(8,128)}, f32[66,8,128]{2,1,0:T(8,128)S(1)}, u32[]{:S(2)}, u32[]{:S(2)}) collective-permute-start(f32[66,8,128]{2,1,0:T(8,128)} %get-tuple-element.14), channel_id=1, source_target_pairs={{0,1},{1,2},{2,3},{3,4},{4,5},{5,6},{6,7},{7,8},{8,9},{9,10},{10,1... | collective-permute-start | bytes 811016 | tf_op jit(solution)/shard_map/ppermute | solution.py:473
  21.2 8.0 %collective-permute-start.4 = (f32[66,8,128]{2,1,0:T(8,128)}, f32[66,8,128]{2,1,0:T(8,128)S(1)}, u32[]{:S(2)}, u32[]{:S(2)}) collective-permute-start(f32[66,8,128]{2,1,0:T(8,128)} %get-tuple-element.15), channel_id=1, source_target_pairs={{1,0},{2,1},{3,2},{4,3},{5,4},{6,5},{7,6},{8,7},{9,8},{10,9},{11,1... | collective-permute-start | bytes 811016 | tf_op jit(solution)/shard_map/ppermute | solution.py:473
  25.2 0.7 %copy-start.5 = (f32[8]{0:T(128)S(1)}, f32[8]{0:T(128)}, u32[]{:S(2)}) copy-start(f32[8]{0:T(128)} %param.17) | copy-start | bytes 100
  25.2 0.7 %copy-start.6 = (f32[8]{0:T(128)S(1)}, f32[8]{0:T(128)}, u32[]{:S(2)}) copy-start(f32[8]{0:T(128)} %param.16) | copy-start | bytes 100
  26.4 2.8 %copy-start.1 = (f32[114,8,128]{2,1,0:T(8,128)}, f32[114,8,128]{2,1,0:T(8,128)S(1)}, u32[]{:S(2)}) copy-start(f32[114,8,128]{2,1,0:T(8,128)S(1)} %collective-permute-done.1.refs_7_) | copy-start | bytes 1400836
  26.5 2.8 %copy-start.2 = (f32[114,8,128]{2,1,0:T(8,128)}, f32[114,8,128]{2,1,0:T(8,128)S(1)}, u32[]{:S(2)}) copy-start(f32[114,8,128]{2,1,0:T(8,128)S(1)} %collective-permute-done.2.refs_8_) | copy-start | bytes 1400836
  26.5 2.8 %copy-start.3 = (f32[66,8,128]{2,1,0:T(8,128)}, f32[66,8,128]{2,1,0:T(8,128)S(1)}, u32[]{:S(2)}) copy-start(f32[66,8,128]{2,1,0:T(8,128)S(1)} %collective-permute-done.3.refs_9_) | copy-start | bytes 811012
  29.2 0.7 %copy-start.4 = (f32[66,8,128]{2,1,0:T(8,128)}, f32[66,8,128]{2,1,0:T(8,128)S(1)}, u32[]{:S(2)}) copy-start(f32[66,8,128]{2,1,0:T(8,128)S(1)} %collective-permute-done.4.refs_10_) | copy-start | bytes 811012

commit v2 on v1

--- a/solution.py
+++ b/solution.py
@@ -99,8 +99,9 @@
         out_ref[64 * e : 64 * e + 64, :] = total.astype(bf16)
 
 
-def pack_kernel(plan, scal, u, v, m, mat, mask, inc, xv, g, to_prev, to_next, *zsends):
+def pack_kernel(plan, u, v, m, mat, mask, inc, xv, g, to_prev, to_next, *zsends):
     Z, Y, H, T = plan.Z, plan.Y, plan.H, plan.T
+    scal = place(plan)
     for z in range(Z):
         for h in range(H):
             lanes = slice(h * LANES, (h + 1) * LANES)
@@ -140,6 +141,12 @@
             zsend[T + i] = xv[first_v + i, :, 4 * Y :, :]
 
 
+def place(plan):
+    depth = lax.axis_index("depth")
+    one = (depth >= 0).astype(jnp.int32)
+    return depth, plan.offset(depth), (depth == plan.D - 1).astype(jnp.int32), one
+
+
 def halo_places(plan, scal):
     if plan.D == 1:
         return []
@@ -168,7 +175,7 @@
             to_next[t] = zrecv[i, h, low : low + 8, :]
 
 
-def main_kernel(plan, scal, tables, imp, weights, xv, gown, *refs):
+def main_kernel(plan, dilations, shears, imp, weights, xv, gown, *refs):
     n = 0 if plan.D == 1 else 1 if plan.swap else 2
     zrecvs, from_prev, from_next = refs[:n], refs[n], refs[n + 1]
     corners = refs[n + 2 : len(refs) - 11]
@@ -176,6 +183,7 @@
     U, V, DM, lam, mu, G, CI, F, KB = refs[len(refs) - 9 :]
     Z, Y, X, H, T = plan.Z, plan.Y, plan.X, plan.H, plan.T
     PB, P0, R, ZB, ZS, YB = plan.PB, plan.P0, plan.hrow, plan.ZB, plan.ZS, plan.YB
+    scal = place(plan)
     offset = scal[1]
     halves = range(H)
     row = lax.broadcasted_iota(jnp.int32, (8, LANES), 0)
@@ -249,7 +257,7 @@
                     V[at_v + i - T, h, at, :] = source[k * len(tiles) + t]
             V[lacks, :, low : low + R, :] = jnp.zeros((H, R, LANES), f32)
 
-    n_levels = tables.shape[1]
+    n_levels = dilations.shape[0]
 
     def prepare(z, carry):
         for h in halves:
@@ -265,8 +273,8 @@
                 she = jnp.zeros((8, LANES), f32)
                 for k in range(n_levels):
                     here = level == float(k + 1)
-                    dil = jnp.where(here, tables[0, k], dil)
-                    she = jnp.where(here, tables[1, k], she)
+                    dil = jnp.where(here, dilations[k], dil)
+                    she = jnp.where(here, shears[k], she)
                 lam[z, h, first : first + 8, :] = dil
                 mu[z, h, first : first + 8, :] = she
         for p in range(PB):
@@ -391,12 +399,10 @@
             for i in range(rows):
                 two_layers(first + i, 0)
 
-        U3 = 3
-        full, rest = count // U3, count % U3
-        if full:
-            lax.fori_loop(0, full * scal[3], lambda i, c: (chunk(U3 * i, U3), c)[1], 0)
-        if rest:
-            lax.fori_loop(0, scal[3], lambda i, c: (chunk(U3 * full, rest), c)[1], 0)
+        straight = count if plan.ZB <= 16 else 1
+        full, rest = count // straight, count % straight
+        lax.fori_loop(0, full * scal[3], lambda i, c: (chunk(straight * i, straight), c)[1], 0)
+        assert rest == 0
 
     for s in range(T):
         one_step(s, s == T - 1)
@@ -421,30 +427,30 @@
 
 def per_device(plan, u, v, m, mat, dilation_table, shear_table, stiffness_pair, impedance, mask, inc):
     Z, Y, X, H, T, D, L = plan.Z, plan.Y, plan.X, plan.H, plan.T, plan.D, plan.L
-    depth = lax.axis_index("depth")
-    scal = jnp.stack(
-        [depth, jnp.asarray(plan.offset(depth)), (depth == D - 1).astype(jnp.int32), jnp.asarray(1)]
-    ).astype(jnp.int32)
     shape = lambda *dims: jax.ShapeDtypeStruct(dims, f32)
 
+    room = pltpu.CompilerParams(vmem_limit_bytes=40 * 2**20)
     rows, cols = selectors()
     weights = pl.pallas_call(
         matrix_kernel,
-        out_shape=jax.ShapeDtypeStruct((256, 256), bf16),
+        out_shape=pltpu.VMEM((256, 256), bf16),
+        compiler_params=room,
         name="matrix",
     )(stiffness_pair.reshape(48, 24), jnp.asarray(rows, bf16), jnp.asarray(cols, bf16))
 
     n_sends = 0 if D == 1 else 1 if plan.swap else 2
     tiles, waves = plan.own_tiles()
-    edge = shape(len(tiles) + len(waves), 8, LANES)
+    local = lambda *dims: pltpu.VMEM(dims, f32)
+    edge = local(len(tiles) + len(waves), 8, LANES)
     packed = pl.pallas_call(
         lambda *refs: pack_kernel(plan, *refs),
-        out_shape=[shape(Z, H, 8 * Y, LANES), shape(T, H, 4 * Y, LANES), edge, edge]
-        + [shape(2 * T - 1, H, 4 * Y, LANES)] * n_sends,
-        in_specs=[smem()] + [vmem()] * 6,
+        out_shape=[local(Z, H, 8 * Y, LANES), local(T, H, 4 * Y, LANES), edge, edge]
+        + [local(2 * T - 1, H, 4 * Y, LANES)] * n_sends,
+        in_specs=[vmem()] * 6,
         out_specs=[vmem()] * (4 + n_sends),
+        compiler_params=room,
         name="pack",
-    )(scal, u, v, m, mat, mask, inc)
+    )(*[pltpu.with_memory_space_constraint(a, pltpu.HBM) for a in (u, v, m, mat, mask, inc)])
     xv, g, to_prev, to_next = packed[:4]
     sends = packed[4:]
     up = [(i + 1, i) for i in range(L - 1)]
@@ -462,16 +468,19 @@
     from_prev = lax.ppermute(to_next, "lat", down)
     corners = []
     if zrecvs:
-        corner = shape(len(zrecvs) * len(plan.corner_tiles()), 8, LANES)
+        corner = local(len(zrecvs) * len(plan.corner_tiles()), 8, LANES)
         corner_prev, corner_next = pl.pallas_call(
             lambda *refs: corner_kernel(plan, *refs),
             out_shape=[corner, corner],
             in_specs=[vmem()] * len(zrecvs),
             out_specs=[vmem()] * 2,
+            compiler_params=room,
             name="corner",
-        )(*zrecvs)
+        )(*[pltpu.with_memory_space_constraint(a, pltpu.VMEM) for a in zrecvs])
         corners = [lax.ppermute(corner_next, "lat", down), lax.ppermute(corner_prev, "lat", up)]
-    tables = jnp.stack([dilation_table, shear_table])
+    near = lambda arrays: [pltpu.with_memory_space_constraint(a, pltpu.VMEM) for a in arrays]
+    zrecvs, corners = near(zrecvs), near(corners)
+    from_prev, from_next, xv, g, weights = near([from_prev, from_next, xv, g, weights])
     grid = (plan.ZS, H, 4 * plan.YB, LANES)
     new_u, new_v = pl.pallas_call(
         lambda *refs: main_kernel(plan, *refs),
@@ -489,8 +498,9 @@
             pltpu.VMEM((plan.PB, 2, H, 8, LANES), f32),
             pltpu.VMEM((2, plan.ZS, plan.PB + 1, 48, X), bf16),
         ],
+        compiler_params=room,
         name="steps",
-    )(scal, tables, impedance, weights, xv, g, *zrecvs, from_prev, from_next, *corners)
+    )(dilation_table, shear_table, impedance, weights, xv, g, *zrecvs, from_prev, from_next, *corners)
     return new_u, new_v
 
 

time: 49.3 us -> 41.4 us (0.84)
  Pallas kernels: 25.4 us -> 17.2 us
  waiting for transfers between devices: 5.16 us -> 7.37 us
  local copies, waits for them, and re-layouts: 2.12 us -> 0.7 us
  other arithmetic: 1.15 us -> 0 us
    pallas_call x1, Pallas kernels: 18.9 us -> 15.4 us  [per_device(): pl.pallas_call(lambda *refs: main_kernel(plan, *refs), out_shape=[shape(3...]
    pallas_call x2, Pallas kernels: 4.6 us -> 1.79 us  [the longest x1 1.33 us: per_device(): pl.pallas_call(lambda *refs: pack_kernel(plan, *refs), out_shape=[local(Z...]
    ppermute x1, waiting for transfers between devices: 0.01 us -> 2.23 us  [per_device(): lax.ppermute(corner_next, 'lat', down)]
    pallas_call x1, Pallas kernels: 1.82 us -> 0.04 us  [per_device(): pl.pallas_call(lambda *refs: corner_kernel(plan, *refs), out_shape=[corne...]
    unnamed x14 -> x12, local copies, waits for them, and re-layouts: 2.12 us -> 0.7 us
    another operation x2 -> x0, other arithmetic: 1.15 us -> none  [the longest x1 0.62 us: per_device(): jnp.stack([depth, jnp.asarray(plan.offset(depth)), (depth == D - 1).astyp...]
  transfers between devices with their start and end apart: 5 -> 5, of which waited for: 2 -> 3; matrix products, arithmetic and copies ran while one was open for 1% -> 0% of each run, Pallas kernels for 8% -> 1%
where the time goes in v2:
time: 41.4 us; the launch traced here: 40.6 us
  Pallas kernels  17.2 us (42%)
  starting transfers between devices  14.6 us (35%)
  waiting for transfers between devices  7.37 us (18%)
  between operations  0.75 us (2%)
  local copies, waits for them, and re-layouts  0.7 us (2%)
    pallas_call x1, Pallas kernels, per_device(): pl.pallas_call(lambda *refs: main_kernel(plan, *refs), out_shape=[shape(3...  15.4 us
    ppermute x1, starting transfers between devices, per_device(): lax.ppermute(corner_next, 'lat', down)  4.53 us
    ppermute x1, starting transfers between devices, per_device(): from_prev = lax.ppermute(to_next, 'lat', down)  3.98 us
    ppermute x1, waiting for transfers between devices, per_device(): lax.ppermute(corner_prev, 'lat', up)  3.1 us
    ppermute x1, waiting for transfers between devices, per_device(): lax.ppermute(corner_next, 'lat', down)  2.23 us
    ppermute x1, starting transfers between devices, per_device(): zrecvs = [lax.ppermute(sends[0], 'depth', [(0, 1), (1, 0)])]  2.09 us
    ppermute x1, starting transfers between devices, per_device(): from_next = lax.ppermute(to_prev, 'lat', up)  2.05 us
    ppermute x1, waiting for transfers between devices, per_device(): zrecvs = [lax.ppermute(sends[0], 'depth', [(0, 1), (1, 0)])]  2.04 us
  transfers between devices with their start and end apart: 5, of which 3 were waited for; matrix products, arithmetic and copies ran while one was open for 0% of the time, Pallas kernels for 1%

profile of v2, /device:TPU:1, one launch (start us, length us, event | category | flops | bytes accessed | tf_op | source)
XLA Modules:
  0.0 40.6 jit_solution(15767254875094595476)
XLA Ops:
  0.6 1.3 %pack.1 = (f32[8,2,64,128]{3,2,1,0:T(8,128)S(1)}, f32[6,2,32,128]{3,2,1,0:T(8,128)S(1)}, f32[114,8,128]{2,1,0:T(8,128)S(1)}, f32[114,8,128]{2,1,0:T(8,128)S(1)}, f32[11,2,32,128]{3,2,1,0:T(8,128)S(1)}) custom-call(f32[3,8,8,256]{3,2,1,0:T(8,128)} %refs_0_.2, f32[3,8,8,256]{3,2,1,0:T(8,128)} %refs_1_.2, f32[8,8,256]{2,1,0:T(8,128)} %refs_2_.2, ...), custom_call_target="tpu_custom_call" | custom-call | tf_op jit(solution)/shard_map/pack/pallas_call | solution.py:445
  2.0 2.1 %collective-permute-start = (f32[11,2,32,128]{3,2,1,0:T(8,128)S(1)}, f32[11,2,32,128]{3,2,1,0:T(8,128)S(1)}, u32[]{:S(2)}, u32[]{:S(2)}) collective-permute-start(f32[11,2,32,128]{3,2,1,0:T(8,128)S(1)} %get-tuple-element.11), channel_id=1, source_target_pairs={{0,16},{16,0},{1,17},{17,1},{2,18},{18,2},{3,19},{19,3},{4,20},{20... | collective-permute-start | bytes 1081352 | tf_op jit(solution)/shard_map/ppermute | solution.py:461
  4.1 4.0 %collective-permute-start.1 = (f32[114,8,128]{2,1,0:T(8,128)S(1)}, f32[114,8,128]{2,1,0:T(8,128)S(1)}, u32[]{:S(2)}, u32[]{:S(2)}) collective-permute-start(f32[114,8,128]{2,1,0:T(8,128)S(1)} %get-tuple-element.12), channel_id=1, source_target_pairs={{0,1},{1,2},{2,3},{3,4},{4,5},{5,6},{6,7},{7,8},{8,9},{9,10},{10,1... | collective-permute-start | bytes 1400840 | tf_op jit(solution)/shard_map/ppermute | solution.py:468
  8.0 0.0 copy-start
  8.1 0.0 copy-start.1
  8.1 0.0 copy-start.2
  8.1 2.1 %collective-permute-start.2 = (f32[114,8,128]{2,1,0:T(8,128)S(1)}, f32[114,8,128]{2,1,0:T(8,128)S(1)}, u32[]{:S(2)}, u32[]{:S(2)}) collective-permute-start(f32[114,8,128]{2,1,0:T(8,128)S(1)} %get-tuple-element.13), channel_id=1, source_target_pairs={{1,0},{2,1},{3,2},{4,3},{5,4},{6,5},{7,6},{8,7},{9,8},{10,9},{11,1... | collective-permute-start | bytes 1400840 | tf_op jit(solution)/shard_map/ppermute | solution.py:467
  10.1 2.0 %collective-permute-done.refs_0_.refs_6_ = f32[11,2,32,128]{3,2,1,0:T(8,128)S(1)} collective-permute-done((f32[11,2,32,128]{3,2,1,0:T(8,128)S(1)}, f32[11,2,32,128]{3,2,1,0:T(8,128)S(1)}, u32[]{:S(2)}, u32[]{:S(2)}) %collective-permute-start) | collective-permute-done | bytes 360480 | tf_op jit(solution)/shard_map/ppermute | solution.py:461
  12.2 4.5 %collective-permute-start.3 = (f32[66,8,128]{2,1,0:T(8,128)S(1)}, f32[66,8,128]{2,1,0:T(8,128)S(1)}, u32[]{:S(2)}, u32[]{:S(2)}) collective-permute-start(f32[66,8,128]{2,1,0:T(8,128)S(1)} %get-tuple-element.14), channel_id=1, source_target_pairs={{0,1},{1,2},{2,3},{3,4},{4,5},{5,6},{6,7},{7,8},{8,9},{9,10},{10,1... | collective-permute-start | bytes 811016 | tf_op jit(solution)/shard_map/ppermute | solution.py:480
  16.8 1.9 %collective-permute-start.4 = (f32[66,8,128]{2,1,0:T(8,128)S(1)}, f32[66,8,128]{2,1,0:T(8,128)S(1)}, u32[]{:S(2)}, u32[]{:S(2)}) collective-permute-start(f32[66,8,128]{2,1,0:T(8,128)S(1)} %get-tuple-element.15), channel_id=1, source_target_pairs={{1,0},{2,1},{3,2},{4,3},{5,4},{6,5},{7,6},{8,7},{9,8},{10,9},{11,1... | collective-permute-start | bytes 811016 | tf_op jit(solution)/shard_map/ppermute | solution.py:480
  18.7 0.0 copy-done
  18.7 0.0 copy-done.1
  18.7 0.0 copy-done.2
  18.7 0.5 %matrix.1.refs_3_ = bf16[256,256]{1,0:T(8,128)(2,1)S(1)} custom-call(f32[48,24]{1,0:T(8,128)S(1)} %bitcast.1, bf16[4,64,48]{2,1,0:T(8,128)(2,1)S(1)} %copy-done.1, bf16[2,4,24,256]{3,2,1,0:T(8,128)(2,1)S(1)} %copy-done), custom_call_target="tpu_custom_call" | custom-call | tf_op jit(solution)/shard_map/matrix/pallas_call | solution.py:434
  19.2 0.0 collective-permute-done.1.refs_7_
  19.2 0.0 collective-permute-done.2.refs_8_
  19.2 2.2 %collective-permute-done.3.refs_9_ = f32[66,8,128]{2,1,0:T(8,128)S(1)} collective-permute-done((f32[66,8,128]{2,1,0:T(8,128)S(1)}, f32[66,8,128]{2,1,0:T(8,128)S(1)}, u32[]{:S(2)}, u32[]{:S(2)}) %collective-permute-start.3) | collective-permute-done | bytes 270368 | tf_op jit(solution)/shard_map/ppermute | solution.py:480
  21.4 3.1 %collective-permute-done.4.refs_10_ = f32[66,8,128]{2,1,0:T(8,128)S(1)} collective-permute-done((f32[66,8,128]{2,1,0:T(8,128)S(1)}, f32[66,8,128]{2,1,0:T(8,128)S(1)}, u32[]{:S(2)}, u32[]{:S(2)}) %collective-permute-start.4) | collective-permute-done | bytes 270368 | tf_op jit(solution)/shard_map/ppermute | solution.py:480
  24.5 0.0 copy-start.3
  24.5 0.0 copy-start.4
  24.5 0.6 %copy-done.3 = f32[8]{0:T(128)S(1)} copy-done((f32[8]{0:T(128)S(1)}, f32[8]{0:T(128)}, u32[]{:S(2)}) %copy-start.3) | copy-done | bytes 56
  25.2 0.0 copy-done.4
  25.2 0.0 copy-done.5
  25.2 15.4 %steps.1 = (f32[3,8,8,256]{3,2,1,0:T(8,128)}, f32[3,8,8,256]{3,2,1,0:T(8,128)}) custom-call(f32[8]{0:T(128)S(1)} %copy-done.3, f32[8]{0:T(128)S(1)} %copy-done.4, f32[3]{0:T(128)S(1)} %copy-done.5, bf16[256,256]{1,0:T(8,128)(2,1)S(1)} %matrix.1.refs_3_, f32[8,2,64,128]{3,2,1,0:T(8,128)S(1)} %get-tuple-element.9.refs_4_, ...), custom_call_target="tpu_custom_call" | custom-call | tf_op jit(solution)/shard_map/steps/pallas_call | solution.py:485
  (2 shorter events, 0.0 us)
Async XLA Ops:
  2.0 10.2 %collective-permute-start = (f32[11,2,32,128]{3,2,1,0:T(8,128)S(1)}, f32[11,2,32,128]{3,2,1,0:T(8,128)S(1)}, u32[]{:S(2)}, u32[]{:S(2)}) collective-permute-start(f32[11,2,32,128]{3,2,1,0:T(8,128)S(1)} %get-tuple-element.11), channel_id=1, source_target_pairs={{0,16},{16,0},{1,17},{17,1},{2,18},{18,2},{3,19},{19,3},{4,20},{20... | collective-permute-start | bytes 1081352 | tf_op jit(solution)/shard_map/ppermute | solution.py:461
  4.1 15.1 %collective-permute-start.1 = (f32[114,8,128]{2,1,0:T(8,128)S(1)}, f32[114,8,128]{2,1,0:T(8,128)S(1)}, u32[]{:S(2)}, u32[]{:S(2)}) collective-permute-start(f32[114,8,128]{2,1,0:T(8,128)S(1)} %get-tuple-element.12), channel_id=1, source_target_pairs={{0,1},{1,2},{2,3},{3,4},{4,5},{5,6},{6,7},{7,8},{8,9},{9,10},{10,1... | collective-permute-start | bytes 1400840 | tf_op jit(solution)/shard_map/ppermute | solution.py:468
  8.0 10.6 %copy-start = (bf16[2,4,24,256]{3,2,1,0:T(8,128)(2,1)S(1)}, bf16[2,4,24,256]{3,2,1,0:T(8,128)(2,1)}, u32[]{:S(2)}) copy-start(bf16[2,4,24,256]{3,2,1,0:T(8,128)(2,1)} %constant.5.clone.cols_ref) | copy-start | bytes 294916
  8.1 10.6 %copy-start.1 = (bf16[4,64,48]{2,1,0:T(8,128)(2,1)S(1)}, bf16[4,64,48]{2,1,0:T(8,128)(2,1)}, u32[]{:S(2)}) copy-start(bf16[4,64,48]{2,1,0:T(8,128)(2,1)} %constant.4.clone.rows_ref) | copy-start | bytes 73732
  8.1 10.6 %copy-start.2 = (f32[2,24,24]{2,1,0:T(8,128)S(1)}, f32[2,24,24]{2,1,0:T(8,128)}, u32[]{:S(2)}) copy-start(f32[2,24,24]{2,1,0:T(8,128)} %param.18) | copy-start | bytes 13828
  8.1 11.1 %collective-permute-start.2 = (f32[114,8,128]{2,1,0:T(8,128)S(1)}, f32[114,8,128]{2,1,0:T(8,128)S(1)}, u32[]{:S(2)}, u32[]{:S(2)}) collective-permute-start(f32[114,8,128]{2,1,0:T(8,128)S(1)} %get-tuple-element.13), channel_id=1, source_target_pairs={{1,0},{2,1},{3,2},{4,3},{5,4},{6,5},{7,6},{8,7},{9,8},{10,9},{11,1... | collective-permute-start | bytes 1400840 | tf_op jit(solution)/shard_map/ppermute | solution.py:467
  12.2 9.2 %collective-permute-start.3 = (f32[66,8,128]{2,1,0:T(8,128)S(1)}, f32[66,8,128]{2,1,0:T(8,128)S(1)}, u32[]{:S(2)}, u32[]{:S(2)}) collective-permute-start(f32[66,8,128]{2,1,0:T(8,128)S(1)} %get-tuple-element.14), channel_id=1, source_target_pairs={{0,1},{1,2},{2,3},{3,4},{4,5},{5,6},{6,7},{7,8},{8,9},{9,10},{10,1... | collective-permute-start | bytes 811016 | tf_op jit(solution)/shard_map/ppermute | solution.py:480
  16.8 7.8 %collective-permute-start.4 = (f32[66,8,128]{2,1,0:T(8,128)S(1)}, f32[66,8,128]{2,1,0:T(8,128)S(1)}, u32[]{:S(2)}, u32[]{:S(2)}) collective-permute-start(f32[66,8,128]{2,1,0:T(8,128)S(1)} %get-tuple-element.15), channel_id=1, source_target_pairs={{1,0},{2,1},{3,2},{4,3},{5,4},{6,5},{7,6},{8,7},{9,8},{10,9},{11,1... | collective-permute-start | bytes 811016 | tf_op jit(solution)/shard_map/ppermute | solution.py:480
  24.5 0.7 %copy-start.3 = (f32[8]{0:T(128)S(1)}, f32[8]{0:T(128)}, u32[]{:S(2)}) copy-start(f32[8]{0:T(128)} %refs_0_.3) | copy-start | bytes 100
  24.5 0.7 %copy-start.4 = (f32[8]{0:T(128)S(1)}, f32[8]{0:T(128)}, u32[]{:S(2)}) copy-start(f32[8]{0:T(128)} %refs_1_.3) | copy-start | bytes 100
  24.5 0.7 %copy-start.5 = (f32[3]{0:T(128)S(1)}, f32[3]{0:T(128)}, u32[]{:S(2)}) copy-start(f32[3]{0:T(128)} %refs_2_.3) | copy-start | bytes 40

commit v3 on v2

--- a/solution.py
+++ b/solution.py
@@ -40,20 +40,67 @@
             return 0
         return depth * self.T if self.swap else self.T
 
+    def halo_tiles(self, u_layers, v_layers):
+        n = self.hy // 2
+        tiles = [("u", z, h, p) for z in u_layers for h in range(self.H) for p in range(n)]
+        tiles += [("v", z, h, p) for z in v_layers for h in range(self.H) for p in range(n - 1)]
+        if self.T % 2 == 0:
+            tiles += [("half", z, h, 0) for z in v_layers for h in range(0, self.H, 2)]
+        return tiles
+
     def own_tiles(self):
-        n = self.hy // 2
-        tiles = [(f, z, h, p) for f in (0, 1) for z in range(self.Z) for h in range(self.H) for p in range(n)]
-        waves = [
+        return self.halo_tiles(range(self.Z), range(self.Z)), [
             (s, h, k, n_pairs)
             for s, n_pairs in enumerate(self.gpairs)
             for h in range(self.H)
             for k in range(n_pairs)
         ]
-        return tiles, waves
 
     def corner_tiles(self):
-        n = self.hy // 2
-        return [(i, h, p) for i in range(2 * self.T - 1) for h in range(self.H) for p in range(n)]
+        return self.halo_tiles(range(self.T), range(self.T, 2 * self.T - 1))
+
+    def sides(self):
+        odd = lax.rem(lax.axis_index("lat"), jnp.int32(2))
+        return odd == 1, odd == 0
+
+
+def aligned(value):
+    return pl.multiple_of(value, 8)
+
+
+def first_half():
+    return lax.broadcasted_iota(jnp.int32, (8, LANES), 0) < 4
+
+
+def put_halo(plan, tiles, out, start, to_next, read):
+    n, R, top = plan.hy // 2, plan.hrow, 4 * plan.Y - plan.hrow
+    u_low = jnp.where(to_next, top, 0)
+    v_low = jnp.where(to_next, top + 8, 0)
+    far = jnp.where(to_next, top, R - 8)
+    for t, (kind, z, h, p) in enumerate(tiles):
+        if kind == "half":
+            a, b = read("v", z, h, aligned(far)), read("v", z, h + 1, aligned(far))
+            low = jnp.where(first_half(), a, pltpu.roll(b, 4, 0))
+            high = jnp.where(first_half(), pltpu.roll(a, 4, 0), b)
+            out[start + t] = jnp.where(to_next, high, low)
+        else:
+            out[start + t] = read(kind, z, h, aligned((u_low if kind == "u" else v_low) + 8 * p))
+
+
+def take_halo(plan, tiles, source, start, from_next, write):
+    n, R = plan.hy // 2, plan.hrow
+    u_low = jnp.where(from_next, R + 4 * plan.Y, 0)
+    v_low = jnp.where(from_next, R + 4 * plan.Y, 8)
+    far = jnp.where(from_next, R + 4 * plan.Y + 8 * (n - 1), 0)
+    for t, (kind, z, h, p) in enumerate(tiles):
+        tile = source[start + t]
+        if kind == "half":
+            turned = pltpu.roll(tile, 4, 0)
+            keep = first_half() == from_next
+            write("v", z, h, aligned(far), jnp.where(keep, jnp.where(from_next, tile, turned), 0.0))
+            write("v", z, h + 1, aligned(far), jnp.where(keep, jnp.where(from_next, turned, tile), 0.0))
+        else:
+            write(kind, z, h, aligned((u_low if kind == "u" else v_low) + 8 * p), tile)
 
 
 def selectors():
@@ -86,7 +133,7 @@
     return rows, cols
 
 
-def matrix_kernel(stiff_ref, rows_ref, cols_ref, out_ref):
+def matrix_kernel(stiff_ref, rows_ref, cols_ref, dilations, shears, imp, out_ref, tiles_ref):
     stiff = stiff_ref[...]
     high = stiff.astype(bf16)
     low = (stiff - high.astype(f32)).astype(bf16)
@@ -97,9 +144,18 @@
             placed = jnp.dot(picked, cols_ref[k, e], preferred_element_type=f32)
             total = placed if total is None else total + placed
         out_ref[64 * e : 64 * e + 64, :] = total.astype(bf16)
-
-
-def pack_kernel(plan, u, v, m, mat, mask, inc, xv, g, to_prev, to_next, *zsends):
+    n = dilations.shape[0]
+    for k in range(n):
+        tiles_ref[k] = jnp.full((8, LANES), dilations[k], f32)
+        tiles_ref[n + k] = jnp.full((8, LANES), shears[k], f32)
+    row = lax.broadcasted_iota(jnp.int32, (8, LANES), 0)
+    wave = jnp.zeros((8, LANES), f32)
+    for c in range(3):
+        wave = jnp.where((row == c) | (row == 4 + c), imp[c], wave)
+    tiles_ref[2 * n] = wave
+
+
+def pack_kernel(plan, u, v, m, mat, mask, inc, xv, g, to_first, to_second, *zsends):
     Z, Y, H, T = plan.Z, plan.Y, plan.H, plan.T
     scal = place(plan)
     for z in range(Z):
@@ -122,13 +178,15 @@
                     g[s, h, pl.ds(4 * y + c, 8, stride=4), :] = double * inc[s, c, rows, lanes]
                 g[s, h, pl.ds(4 * y + 3, 8, stride=4), :] = jnp.zeros((8, LANES), f32)
     tiles, waves = plan.own_tiles()
-    for out, low in ((to_prev, 0), (to_next, 4 * Y - plan.hrow)):
-        for t, (f, z, h, p) in enumerate(tiles):
-            at = 4 * Y * f + low + 8 * p
-            out[t] = xv[z, h, at : at + 8, :]
+
+    def read(kind, z, h, row):
+        return xv[z, h, pl.ds(row + (4 * Y if kind == "v" else 0), 8), :]
+
+    for out, to_next in zip((to_first, to_second), plan.sides()):
+        put_halo(plan, tiles, out, 0, to_next, read)
         for t, (s, h, k, n_pairs) in enumerate(waves):
-            at = 8 * k if low == 0 else 4 * Y - 8 * n_pairs + 8 * k
-            out[len(tiles) + t] = g[s, h, at : at + 8, :]
+            at = aligned(jnp.where(to_next, 4 * Y - 8 * n_pairs, 0) + 8 * k)
+            out[len(tiles) + t] = g[s, h, pl.ds(at, 8), :]
     for k, zsend in enumerate(zsends):
         if plan.swap:
             first = jnp.where(scal[0] == 0, Z - T, 0)
@@ -165,22 +223,24 @@
 
 def corner_kernel(plan, *refs):
     n = len(refs) - 2
-    zrecvs, (to_prev, to_next) = refs[:n], refs[n:]
+    zrecvs, outs = refs[:n], refs[n:]
     tiles = plan.corner_tiles()
-    for k, zrecv in enumerate(zrecvs):
-        for t, (i, h, p) in enumerate(tiles):
-            t += k * len(tiles)
-            to_prev[t] = zrecv[i, h, 8 * p : 8 * p + 8, :]
-            low = 4 * plan.Y - plan.hrow + 8 * p
-            to_next[t] = zrecv[i, h, low : low + 8, :]
-
-
-def main_kernel(plan, dilations, shears, imp, weights, xv, gown, *refs):
+    for out, to_next in zip(outs, plan.sides()):
+        for k, zrecv in enumerate(zrecvs):
+
+            def read(kind, i, h, row):
+                return zrecv[i, h, pl.ds(row, 8), :]
+
+            put_halo(plan, tiles, out, k * len(tiles), to_next, read)
+
+
+def main_kernel(plan, tables, weights, xv, gown, *refs):
     n = 0 if plan.D == 1 else 1 if plan.swap else 2
-    zrecvs, from_prev, from_next = refs[:n], refs[n], refs[n + 1]
+    zrecvs, firsts = refs[:n], refs[n : n + 2]
     corners = refs[n + 2 : len(refs) - 11]
     out_u, out_v = refs[len(refs) - 11 : len(refs) - 9]
     U, V, DM, lam, mu, G, CI, F, KB = refs[len(refs) - 9 :]
+    sides = plan.sides()
     Z, Y, X, H, T = plan.Z, plan.Y, plan.X, plan.H, plan.T
     PB, P0, R, ZB, ZS, YB = plan.PB, plan.P0, plan.hrow, plan.ZB, plan.ZS, plan.YB
     scal = place(plan)
@@ -188,7 +248,7 @@
     halves = range(H)
     row = lax.broadcasted_iota(jnp.int32, (8, LANES), 0)
     lane = lax.broadcasted_iota(jnp.int32, (8, LANES), 1)
-    first_half = row < 4
+    low_half = row < 4
     spare = (row == 3) | (row == 7)
     zero = jnp.zeros((8, LANES), f32)
 
@@ -205,8 +265,8 @@
         tiles = []
         for h in halves:
             swapped = pltpu.roll(ahead[h], 4, 0)
-            even = jnp.where(first_half, parts[h], swapped)
-            odd = jnp.where(first_half, swapped, parts[h])
+            even = jnp.where(low_half, parts[h], swapped)
+            odd = jnp.where(low_half, swapped, parts[h])
             high0 = even.astype(bf16).astype(f32)
             high1 = odd.astype(bf16).astype(f32)
             tiles.append(
@@ -233,31 +293,35 @@
             U[at_u + i, :, mid, :] = zrecv[i]
         for i in range(T - 1):
             V[at_v + i, :, mid, :] = zrecv[T + i]
-        V[lacks, :, mid, :] = jnp.zeros((H, 4 * Y, LANES), f32)
     U[ZB:, :, :, :] = jnp.zeros((ZS - ZB, H, 4 * YB, LANES), f32)
     V[ZB:, :, :, :] = jnp.zeros((ZS - ZB, H, 4 * YB, LANES), f32)
     for s in range(T):
         G[s] = jnp.zeros((H, 4 * YB, LANES), f32)
         G[s, :, mid, :] = gown[s]
     own, waves = plan.own_tiles()
-    for source, low in ((from_prev, 0), (from_next, R + 4 * Y)):
-        for t, (f, z, h, p) in enumerate(own):
-            (V if f else U)[offset + z, h, low + 8 * p : low + 8 * p + 8, :] = source[t]
+    for source, from_next in zip(firsts, sides):
+
+        def write(kind, z, h, row, tile):
+            (U if kind == "u" else V)[offset + z, h, pl.ds(row, 8), :] = tile
+
+        take_halo(plan, own, source, 0, from_next, write)
         for t, (s, h, k, n_pairs) in enumerate(waves):
-            at = (R - 8 * n_pairs if low == 0 else low) + 8 * k
-            G[s, h, at : at + 8, :] = source[len(own) + t]
+            at = aligned(jnp.where(from_next, R + 4 * Y, R - 8 * n_pairs) + 8 * k)
+            G[s, h, pl.ds(at, 8), :] = source[len(own) + t]
     tiles = plan.corner_tiles()
     for k, (at_u, at_v, lacks) in enumerate(halo_places(plan, scal)):
-        for source, low in zip(corners, (0, R + 4 * Y)):
-            for t, (i, h, p) in enumerate(tiles):
-                at = slice(low + 8 * p, low + 8 * p + 8)
-                if i < T:
-                    U[at_u + i, h, at, :] = source[k * len(tiles) + t]
+        for source, from_next in zip(corners, sides):
+
+            def write(kind, i, h, row, tile):
+                if kind == "u":
+                    U[at_u + i, h, pl.ds(row, 8), :] = tile
                 else:
-                    V[at_v + i - T, h, at, :] = source[k * len(tiles) + t]
-            V[lacks, :, low : low + R, :] = jnp.zeros((H, R, LANES), f32)
-
-    n_levels = dilations.shape[0]
+                    V[at_v + i - T, h, pl.ds(row, 8), :] = tile
+
+            take_halo(plan, tiles, source, k * len(tiles), from_next, write)
+        V[lacks, :, :, :] = jnp.zeros((H, 4 * YB, LANES), f32)
+
+    n_levels = tables.shape[0] // 2
 
     def prepare(z, carry):
         for h in halves:
@@ -273,8 +337,8 @@
                 she = jnp.zeros((8, LANES), f32)
                 for k in range(n_levels):
                     here = level == float(k + 1)
-                    dil = jnp.where(here, dilations[k], dil)
-                    she = jnp.where(here, shears[k], she)
+                    dil = jnp.where(here, tables[k], dil)
+                    she = jnp.where(here, tables[n_levels + k], she)
                 lam[z, h, first : first + 8, :] = dil
                 mu[z, h, first : first + 8, :] = she
         for p in range(PB):
@@ -282,22 +346,27 @@
             for h in halves:
                 v = V[z, h, at, :]
                 mass = jnp.where(
-                    first_half,
+                    low_half,
                     jnp.broadcast_to(v[3:4, :], (8, LANES)),
                     jnp.broadcast_to(v[7:8, :], (8, LANES)),
                 )
                 DM[z, h, at, :] = jnp.where(spare, 0.0, time_step * mass)
-            put_columns((0, 1), z, p, [U[z, h, at, :] for h in halves])
+            put_columns((0,), z, p, [U[z, h, at, :] for h in halves])
         for b in range(2):
-            KB[b, z, PB] = jnp.zeros((48, X), bf16)
+            for p in range(widest_pair + 1 if b else PB, PB + 1):
+                KB[b, z, p] = jnp.zeros((48, X), bf16)
         return carry
 
-    lax.fori_loop(0, ZS, prepare, 0)
+    widest_pair = (plan.hy + Y + T - 2) // 2
+    lax.fori_loop(0, ZB, prepare, 0)
+    for z in range(ZB, ZS):
+        for b in range(2):
+            KB[b, z] = jnp.zeros((PB + 1, 48, X), bf16)
+        for ref in (DM, lam, mu):
+            ref[z] = jnp.zeros(ref.shape[1:], f32)
 
     bottom = offset + Z - 1
-    wave = jnp.zeros((8, LANES), f32)
-    for c in range(3):
-        wave = jnp.where((row == c) | (row == 4 + c), imp[c], wave)
+    wave = tables[2 * n_levels]
     wave = jnp.where(scal[2] == 1, wave, zero)
     for h in halves:
         for p in range(PB):
@@ -330,12 +399,12 @@
         def finish(z, p, g0, g1):
             at = slice(8 * p, 8 * p + 8)
             other = [
-                pltpu.roll(jnp.where(first_half, g1[h], g0[h]), 4, 0) for h in halves
+                pltpu.roll(jnp.where(low_half, g1[h], g0[h]), 4, 0) for h in halves
             ]
             other = shift_right(other)
             fresh = []
             for h in halves:
-                force = jnp.where(first_half, g0[h], g1[h]) + other[h]
+                force = jnp.where(low_half, g0[h], g1[h]) + other[h]
                 v = V[z, h, at, :] - DM[z, h, at, :] * force
                 u = U[z, h, at, :] + time_step * v
                 V[z, h, at, :] = v
@@ -431,12 +500,22 @@
 
     room = pltpu.CompilerParams(vmem_limit_bytes=40 * 2**20)
     rows, cols = selectors()
-    weights = pl.pallas_call(
+    n_tables = 2 * dilation_table.shape[0] + 1
+    weights, tables = pl.pallas_call(
         matrix_kernel,
-        out_shape=pltpu.VMEM((256, 256), bf16),
+        out_shape=[pltpu.VMEM((256, 256), bf16), pltpu.VMEM((n_tables, 8, LANES), f32)],
+        in_specs=[vmem()] * 3 + [smem()] * 3,
+        out_specs=[vmem()] * 2,
         compiler_params=room,
         name="matrix",
-    )(stiffness_pair.reshape(48, 24), jnp.asarray(rows, bf16), jnp.asarray(cols, bf16))
+    )(
+        stiffness_pair.reshape(48, 24),
+        jnp.asarray(rows, bf16),
+        jnp.asarray(cols, bf16),
+        dilation_table,
+        shear_table,
+        impedance,
+    )
 
     n_sends = 0 if D == 1 else 1 if plan.swap else 2
     tiles, waves = plan.own_tiles()
@@ -451,10 +530,13 @@
         compiler_params=room,
         name="pack",
     )(*[pltpu.with_memory_space_constraint(a, pltpu.HBM) for a in (u, v, m, mat, mask, inc)])
-    xv, g, to_prev, to_next = packed[:4]
+    xv, g, to_first, to_second = packed[:4]
     sends = packed[4:]
-    up = [(i + 1, i) for i in range(L - 1)]
-    down = [(i, i + 1) for i in range(L - 1)]
+
+    def trade(array, start):
+        pairs = [(i, i + 1) for i in range(start, L - 1, 2)]
+        return lax.ppermute(array, "lat", pairs + [(j, i) for i, j in pairs])
+
     if D == 1:
         zrecvs = []
     elif plan.swap:
@@ -464,12 +546,11 @@
             lax.ppermute(sends[0], "depth", [(i, i + 1) for i in range(D - 1)]),
             lax.ppermute(sends[1], "depth", [(i + 1, i) for i in range(D - 1)]),
         ]
-    from_next = lax.ppermute(to_prev, "lat", up)
-    from_prev = lax.ppermute(to_next, "lat", down)
+    firsts = [trade(to_first, 1), trade(to_second, 0)]
     corners = []
     if zrecvs:
         corner = local(len(zrecvs) * len(plan.corner_tiles()), 8, LANES)
-        corner_prev, corner_next = pl.pallas_call(
+        corner_first, corner_second = pl.pallas_call(
             lambda *refs: corner_kernel(plan, *refs),
             out_shape=[corner, corner],
             in_specs=[vmem()] * len(zrecvs),
@@ -477,15 +558,15 @@
             compiler_params=room,
             name="corner",
         )(*[pltpu.with_memory_space_constraint(a, pltpu.VMEM) for a in zrecvs])
-        corners = [lax.ppermute(corner_next, "lat", down), lax.ppermute(corner_prev, "lat", up)]
+        corners = [trade(corner_first, 1), trade(corner_second, 0)]
     near = lambda arrays: [pltpu.with_memory_space_constraint(a, pltpu.VMEM) for a in arrays]
     zrecvs, corners = near(zrecvs), near(corners)
-    from_prev, from_next, xv, g, weights = near([from_prev, from_next, xv, g, weights])
+    first, second, xv, g, weights, tables = near([*firsts, xv, g, weights, tables])
     grid = (plan.ZS, H, 4 * plan.YB, LANES)
     new_u, new_v = pl.pallas_call(
         lambda *refs: main_kernel(plan, *refs),
         out_shape=[shape(3, Z, Y, X)] * 2,
-        in_specs=[smem()] * 3 + [vmem()] * (5 + len(zrecvs) + len(corners)),
+        in_specs=[vmem()] * (6 + len(zrecvs) + len(corners)),
         out_specs=[vmem()] * 2,
         scratch_shapes=[
             pltpu.VMEM(grid, f32),
@@ -500,7 +581,7 @@
         ],
         compiler_params=room,
         name="steps",
-    )(dilation_table, shear_table, impedance, weights, xv, g, *zrecvs, from_prev, from_next, *corners)
+    )(tables, weights, xv, g, *zrecvs, first, second, *corners)
     return new_u, new_v
 
 

time: 41.4 us -> 38 us (0.918); the launches traced: 40.6 us -> 37.8 us
  starting transfers between devices: 14.6 us -> 10.8 us
  waiting for transfers between devices: 7.37 us -> 8.72 us
    ppermute x4, starting transfers between devices: 12.5 us -> 8.66 us  [trade(): return lax.ppermute(array, 'lat', pairs + [(j, i) for i, j in pairs])]
    ppermute x1, waiting for transfers between devices: 2.04 us -> 4.01 us  [per_device(): zrecvs = [lax.ppermute(sends[0], 'depth', [(0, 1), (1, 0)])]]
    pallas_call x1, Pallas kernels: 15.4 us -> 14.6 us  [per_device(): pl.pallas_call(lambda *refs: main_kernel(plan, *refs), out_shape=[shape(3...]
    ppermute x4, waiting for transfers between devices: 5.34 us -> 4.71 us  [trade(): return lax.ppermute(array, 'lat', pairs + [(j, i) for i, j in pairs])]
    pallas_call x1, Pallas kernels: 0.46 us -> 1.01 us  [per_device(): pl.pallas_call(matrix_kernel, out_shape=[pltpu.VMEM((256, 256), bf16), pl...]
  transfers between devices with their start and end apart: 5 -> 5, of which waited for: 3 -> 3; matrix products, arithmetic and copies ran while one was open for 0% -> 0% of each run, Pallas kernels for 1% -> 3%
where the time goes in v3:
time: 38 us; the launch traced here: 37.8 us
  Pallas kernels  17 us (45%)
  starting transfers between devices  10.8 us (28%)
  waiting for transfers between devices  8.72 us (23%)
  between operations  0.76 us (2%)
  local copies, waits for them, and re-layouts  0.58 us (2%)
    pallas_call x1, Pallas kernels, per_device(): pl.pallas_call(lambda *refs: main_kernel(plan, *refs), out_shape=[shape(3...  14.6 us
    ppermute x4, starting transfers between devices, trade(): return lax.ppermute(array, 'lat', pairs + [(j, i) for i, j in pairs])  8.66 us
    ppermute x4, waiting for transfers between devices, trade(): return lax.ppermute(array, 'lat', pairs + [(j, i) for i, j in pairs])  4.71 us
    ppermute x1, waiting for transfers between devices, per_device(): zrecvs = [lax.ppermute(sends[0], 'depth', [(0, 1), (1, 0)])]  4.01 us
    ppermute x1, starting transfers between devices, per_device(): zrecvs = [lax.ppermute(sends[0], 'depth', [(0, 1), (1, 0)])]  2.09 us
    pallas_call x1, Pallas kernels, per_device(): pl.pallas_call(lambda *refs: pack_kernel(plan, *refs), out_shape=[local(Z...  1.33 us
    pallas_call x1, Pallas kernels, per_device(): pl.pallas_call(matrix_kernel, out_shape=[pltpu.VMEM((256, 256), bf16), pl...  1.01 us
  transfers between devices with their start and end apart: 5, of which 3 were waited for; matrix products, arithmetic and copies ran while one was open for 0% of the time, Pallas kernels for 3%

profile of v3, /device:TPU:1, one launch (start us, length us, event | category | flops | bytes accessed | tf_op | source)
XLA Modules:
  0.0 37.8 jit_solution(696001778611229673)
XLA Ops:
  0.6 1.3 %pack.1 = (f32[8,2,64,128]{3,2,1,0:T(8,128)S(1)}, f32[6,2,32,128]{3,2,1,0:T(8,128)S(1)}, f32[106,8,128]{2,1,0:T(8,128)S(1)}, f32[106,8,128]{2,1,0:T(8,128)S(1)}, f32[11,2,32,128]{3,2,1,0:T(8,128)S(1)}) custom-call(f32[3,8,8,256]{3,2,1,0:T(8,128)} %refs_0_.1, f32[3,8,8,256]{3,2,1,0:T(8,128)} %refs_1_.1, f32[8,8,256]{2,1,0:T(8,128)} %refs_2_.1, ...), custom_call_target="tpu_custom_call" | custom-call | tf_op jit(solution)/shard_map/pack/pallas_call | solution.py:524
  2.0 2.1 %collective-permute-start = (f32[11,2,32,128]{3,2,1,0:T(8,128)S(1)}, f32[11,2,32,128]{3,2,1,0:T(8,128)S(1)}, u32[]{:S(2)}, u32[]{:S(2)}) collective-permute-start(f32[11,2,32,128]{3,2,1,0:T(8,128)S(1)} %get-tuple-element.15), channel_id=1, source_target_pairs={{0,16},{16,0},{1,17},{17,1},{2,18},{18,2},{3,19},{19,3},{4,20},{20... | collective-permute-start | bytes 1081352 | tf_op jit(solution)/shard_map/ppermute | solution.py:543
  4.1 4.0 %collective-permute-start.1 = (f32[106,8,128]{2,1,0:T(8,128)S(1)}, f32[106,8,128]{2,1,0:T(8,128)S(1)}, u32[]{:S(2)}, u32[]{:S(2)}) collective-permute-start(f32[106,8,128]{2,1,0:T(8,128)S(1)} %get-tuple-element.16), channel_id=1, source_target_pairs={{1,2},{3,4},{5,6},{7,8},{9,10},{11,12},{13,14},{2,1},{4,3},{6,5},{... | collective-permute-start | bytes 1302536 | tf_op jit(solution)/shard_map/ppermute | solution.py:538
  8.0 0.0 copy-start
  8.1 0.0 copy-start.1
  8.1 0.0 copy-start.2
  8.1 0.1 collective-permute-start.2
  8.2 4.0 %collective-permute-done.refs_0_.refs_4_ = f32[11,2,32,128]{3,2,1,0:T(8,128)S(1)} collective-permute-done((f32[11,2,32,128]{3,2,1,0:T(8,128)S(1)}, f32[11,2,32,128]{3,2,1,0:T(8,128)S(1)}, u32[]{:S(2)}, u32[]{:S(2)}) %collective-permute-start) | collective-permute-done | bytes 360480 | tf_op jit(solution)/shard_map/ppermute | solution.py:543
  12.2 4.5 %collective-permute-start.3 = (f32[61,8,128]{2,1,0:T(8,128)S(1)}, f32[61,8,128]{2,1,0:T(8,128)S(1)}, u32[]{:S(2)}, u32[]{:S(2)}) collective-permute-start(f32[61,8,128]{2,1,0:T(8,128)S(1)} %get-tuple-element.18), channel_id=1, source_target_pairs={{1,2},{3,4},{5,6},{7,8},{9,10},{11,12},{13,14},{2,1},{4,3},{6,5},{... | collective-permute-start | bytes 749576 | tf_op jit(solution)/shard_map/ppermute | solution.py:538
  16.8 0.0 copy-start.3
  16.8 0.0 copy-start.4
  16.8 0.0 copy-start.5
  16.8 0.1 collective-permute-start.4
  16.9 0.0 copy-done
  16.9 0.0 copy-done.1
  16.9 0.5 %copy-done.3 = f32[8]{0:T(128)S(1)} copy-done((f32[8]{0:T(128)S(1)}, f32[8]{0:T(128)}, u32[]{:S(2)}) %copy-start.3) | copy-done | bytes 56
  17.4 0.0 copy-done.4
  17.4 0.0 copy-done.5
  17.5 1.0 %matrix.1 = (bf16[256,256]{1,0:T(8,128)(2,1)S(1)}, f32[17,8,128]{2,1,0:T(8,128)S(1)}) custom-call(f32[48,24]{1,0:T(8,128)S(1)} %bitcast.1, bf16[4,64,48]{2,1,0:T(8,128)(2,1)S(1)} %copy-done.1, bf16[2,4,24,256]{3,2,1,0:T(8,128)(2,1)S(1)} %copy-done, f32[8]{0:T(128)S(1)} %copy-done.3, f32[8]{0:T(128)S(1)} %copy-done.4, f32[3]{0:T(128)S(1)} %copy-done.5), custom_call_target="tpu_custom_call" | custom-call | tf_op jit(solution)/shard_map/matrix/pallas_call | solution.py:504
  18.5 2.0 %collective-permute-done.1.refs_5_ = f32[106,8,128]{2,1,0:T(8,128)S(1)} collective-permute-done((f32[106,8,128]{2,1,0:T(8,128)S(1)}, f32[106,8,128]{2,1,0:T(8,128)S(1)}, u32[]{:S(2)}, u32[]{:S(2)}) %collective-permute-start.1) | collective-permute-done | bytes 434208 | tf_op jit(solution)/shard_map/ppermute | solution.py:538
  20.5 0.0 collective-permute-done.2.refs_6_
  20.5 2.7 %collective-permute-done.3.refs_7_ = f32[61,8,128]{2,1,0:T(8,128)S(1)} collective-permute-done((f32[61,8,128]{2,1,0:T(8,128)S(1)}, f32[61,8,128]{2,1,0:T(8,128)S(1)}, u32[]{:S(2)}, u32[]{:S(2)}) %collective-permute-start.3) | collective-permute-done | bytes 249888 | tf_op jit(solution)/shard_map/ppermute | solution.py:538
  23.2 0.0 collective-permute-done.4.refs_8_
  23.2 14.6 %steps.1 = (f32[3,8,8,256]{3,2,1,0:T(8,128)}, f32[3,8,8,256]{3,2,1,0:T(8,128)}) custom-call(f32[17,8,128]{2,1,0:T(8,128)S(1)} %get-tuple-element.11.refs_0_, bf16[256,256]{1,0:T(8,128)(2,1)S(1)} %get-tuple-element.12.refs_1_, f32[8,2,64,128]{3,2,1,0:T(8,128)S(1)} %get-tuple-element.13.refs_2_, f32[6,2,32,128]{3,2,1,0:T(8,128)S(1)} %get-tuple-element.14.refs_3_, ...), custom_call_target="tpu_custom_call" | custom-call | tf_op jit(solution)/shard_map/steps/pallas_call | solution.py:566
  (2 shorter events, 0.0 us)
Async XLA Ops:
  2.0 10.2 %collective-permute-start = (f32[11,2,32,128]{3,2,1,0:T(8,128)S(1)}, f32[11,2,32,128]{3,2,1,0:T(8,128)S(1)}, u32[]{:S(2)}, u32[]{:S(2)}) collective-permute-start(f32[11,2,32,128]{3,2,1,0:T(8,128)S(1)} %get-tuple-element.15), channel_id=1, source_target_pairs={{0,16},{16,0},{1,17},{17,1},{2,18},{18,2},{3,19},{19,3},{4,20},{20... | collective-permute-start | bytes 1081352 | tf_op jit(solution)/shard_map/ppermute | solution.py:543
  4.1 16.5 %collective-permute-start.1 = (f32[106,8,128]{2,1,0:T(8,128)S(1)}, f32[106,8,128]{2,1,0:T(8,128)S(1)}, u32[]{:S(2)}, u32[]{:S(2)}) collective-permute-start(f32[106,8,128]{2,1,0:T(8,128)S(1)} %get-tuple-element.16), channel_id=1, source_target_pairs={{1,2},{3,4},{5,6},{7,8},{9,10},{11,12},{13,14},{2,1},{4,3},{6,5},{... | collective-permute-start | bytes 1302536 | tf_op jit(solution)/shard_map/ppermute | solution.py:538
  8.0 8.8 %copy-start = (bf16[2,4,24,256]{3,2,1,0:T(8,128)(2,1)S(1)}, bf16[2,4,24,256]{3,2,1,0:T(8,128)(2,1)}, u32[]{:S(2)}) copy-start(bf16[2,4,24,256]{3,2,1,0:T(8,128)(2,1)} %constant.5.clone.cols_ref) | copy-start | bytes 294916
  8.1 8.8 %copy-start.1 = (bf16[4,64,48]{2,1,0:T(8,128)(2,1)S(1)}, bf16[4,64,48]{2,1,0:T(8,128)(2,1)}, u32[]{:S(2)}) copy-start(bf16[4,64,48]{2,1,0:T(8,128)(2,1)} %constant.4.clone.rows_ref) | copy-start | bytes 73732
  8.1 8.8 %copy-start.2 = (f32[2,24,24]{2,1,0:T(8,128)S(1)}, f32[2,24,24]{2,1,0:T(8,128)}, u32[]{:S(2)}) copy-start(f32[2,24,24]{2,1,0:T(8,128)} %param.18) | copy-start | bytes 13828
  8.1 12.4 %collective-permute-start.2 = (f32[106,8,128]{2,1,0:T(8,128)S(1)}, f32[106,8,128]{2,1,0:T(8,128)S(1)}, u32[]{:S(2)}, u32[]{:S(2)}) collective-permute-start(f32[106,8,128]{2,1,0:T(8,128)S(1)} %get-tuple-element.17), channel_id=1, source_target_pairs={{0,1},{2,3},{4,5},{6,7},{8,9},{10,11},{12,13},{14,15},{1,0},{3,2},... | collective-permute-start | bytes 1302536 | tf_op jit(solution)/shard_map/ppermute | solution.py:538
  12.2 11.0 %collective-permute-start.3 = (f32[61,8,128]{2,1,0:T(8,128)S(1)}, f32[61,8,128]{2,1,0:T(8,128)S(1)}, u32[]{:S(2)}, u32[]{:S(2)}) collective-permute-start(f32[61,8,128]{2,1,0:T(8,128)S(1)} %get-tuple-element.18), channel_id=1, source_target_pairs={{1,2},{3,4},{5,6},{7,8},{9,10},{11,12},{13,14},{2,1},{4,3},{6,5},{... | collective-permute-start | bytes 749576 | tf_op jit(solution)/shard_map/ppermute | solution.py:538
  16.8 0.7 %copy-start.3 = (f32[8]{0:T(128)S(1)}, f32[8]{0:T(128)}, u32[]{:S(2)}) copy-start(f32[8]{0:T(128)} %dilations.1) | copy-start | bytes 100
  16.8 0.7 %copy-start.4 = (f32[8]{0:T(128)S(1)}, f32[8]{0:T(128)}, u32[]{:S(2)}) copy-start(f32[8]{0:T(128)} %shears.1) | copy-start | bytes 100
  16.8 0.7 %copy-start.5 = (f32[3]{0:T(128)S(1)}, f32[3]{0:T(128)}, u32[]{:S(2)}) copy-start(f32[3]{0:T(128)} %imp.1) | copy-start | bytes 40
  16.8 6.4 %collective-permute-start.4 = (f32[61,8,128]{2,1,0:T(8,128)S(1)}, f32[61,8,128]{2,1,0:T(8,128)S(1)}, u32[]{:S(2)}, u32[]{:S(2)}) collective-permute-start(f32[61,8,128]{2,1,0:T(8,128)S(1)} %get-tuple-element.19), channel_id=1, source_target_pairs={{0,1},{2,3},{4,5},{6,7},{8,9},{10,11},{12,13},{14,15},{1,0},{3,2},... | collective-permute-start | bytes 749576 | tf_op jit(solution)/shard_map/ppermute | solution.py:538

commit v4 on v3

--- a/solution.py
+++ b/solution.py
@@ -31,7 +31,6 @@
         self.swap = self.D == 2
         self.ZB = self.Z + (0 if self.D == 1 else T if self.swap else 2 * T)
         self.ZS = self.ZB + 2
-        self.YL = -(-self.YB // 8) * 8
         self.gpairs = [-(-(T - 1 - s) // 2) for s in range(T)]
         self.hrow = 4 * self.hy
 
@@ -105,7 +104,7 @@
 
 def selectors():
     rows = np.zeros((4, 64, 48), np.float32)
-    cols = np.zeros((2, 4, 24, 256), np.float32)
+    cols = np.zeros((2, 4, 24, 240), np.float32)
 
     def half(parity, dx):
         return 4 * (dx ^ parity)
@@ -234,56 +233,80 @@
             put_halo(plan, tiles, out, k * len(tiles), to_next, read)
 
 
-def main_kernel(plan, tables, weights, xv, gown, *refs):
-    n = 0 if plan.D == 1 else 1 if plan.swap else 2
+def column_tiles(plan, parts):
+    ahead = shift_left(plan, parts)
+    tiles = []
+    for h in range(plan.H):
+        swapped = pltpu.roll(ahead[h], 4, 0)
+        even = jnp.where(first_half(), parts[h], swapped)
+        odd = jnp.where(first_half(), swapped, parts[h])
+        high0 = even.astype(bf16).astype(f32)
+        high1 = odd.astype(bf16).astype(f32)
+        tiles.append(
+            (
+                jnp.concatenate([high0, even - high0], 0).astype(bf16),
+                jnp.concatenate([high0, high1], 0).astype(bf16),
+                jnp.concatenate([high1, odd - high1], 0).astype(bf16),
+            )
+        )
+    return tiles
+
+
+def put_columns(plan, columns, z, p, parts):
+    for h, tiles in enumerate(column_tiles(plan, parts)):
+        for j in range(3):
+            columns[z, p, 16 * j : 16 * j + 16, h * LANES : (h + 1) * LANES] = tiles[j]
+
+
+def shift_left(plan, parts):
+    lane = lax.broadcasted_iota(jnp.int32, (8, LANES), 1)
+    rolled = [pltpu.roll(p, LANES - 1, 1) for p in parts] + [jnp.zeros((8, LANES), f32)]
+    return [jnp.where(lane == LANES - 1, rolled[h + 1], rolled[h]) for h in range(plan.H)]
+
+
+def shift_right(plan, parts):
+    lane = lax.broadcasted_iota(jnp.int32, (8, LANES), 1)
+    rolled = [jnp.zeros((8, LANES), f32)] + [pltpu.roll(p, 1, 1) for p in parts]
+    return [jnp.where(lane == 0, rolled[h], rolled[h + 1]) for h in range(plan.H)]
+
+
+def prepare(plan, tables, U, V, DM, lam, mu, columns, z, pairs, level_rows):
+    n_levels = tables.shape[0] // 2
+    row = lax.broadcasted_iota(jnp.int32, (8, LANES), 0)
+    spare = (row == 3) | (row == 7)
+    for h in range(plan.H):
+        for first in level_rows:
+            level = U[z, h, pl.ds(4 * first + 3, 8, stride=4), :]
+            dil = jnp.zeros((8, LANES), f32)
+            she = jnp.zeros((8, LANES), f32)
+            for k in range(n_levels):
+                here = level == float(k + 1)
+                dil = jnp.where(here, tables[k], dil)
+                she = jnp.where(here, tables[n_levels + k], she)
+            lam[z, h, first : first + 8, :] = dil
+            mu[z, h, first : first + 8, :] = she
+    for p in pairs:
+        at = slice(8 * p, 8 * p + 8)
+        for h in range(plan.H):
+            v = V[z, h, at, :]
+            mass = jnp.where(
+                first_half(),
+                jnp.broadcast_to(v[3:4, :], (8, LANES)),
+                jnp.broadcast_to(v[7:8, :], (8, LANES)),
+            )
+            DM[z, h, at, :] = jnp.where(spare, 0.0, time_step * mass)
+        put_columns(plan, columns, z, p, [U[z, h, at, :] for h in range(plan.H)])
+
+
+def begin_kernel(plan, tables, xv, gown, *refs):
+    n = len(refs) - 9
     zrecvs, firsts = refs[:n], refs[n : n + 2]
-    corners = refs[n + 2 : len(refs) - 11]
-    out_u, out_v = refs[len(refs) - 11 : len(refs) - 9]
-    U, V, DM, lam, mu, G, CI, F, KB = refs[len(refs) - 9 :]
-    sides = plan.sides()
+    U, V, DM, lam, mu, G, columns = refs[n + 2 :]
     Z, Y, X, H, T = plan.Z, plan.Y, plan.X, plan.H, plan.T
     PB, P0, R, ZB, ZS, YB = plan.PB, plan.P0, plan.hrow, plan.ZB, plan.ZS, plan.YB
     scal = place(plan)
     offset = scal[1]
-    halves = range(H)
-    row = lax.broadcasted_iota(jnp.int32, (8, LANES), 0)
-    lane = lax.broadcasted_iota(jnp.int32, (8, LANES), 1)
-    low_half = row < 4
-    spare = (row == 3) | (row == 7)
-    zero = jnp.zeros((8, LANES), f32)
-
-    def shift_left(parts):
-        rolled = [pltpu.roll(p, LANES - 1, 1) for p in parts] + [zero]
-        return [jnp.where(lane == LANES - 1, rolled[h + 1], rolled[h]) for h in halves]
-
-    def shift_right(parts):
-        rolled = [zero] + [pltpu.roll(p, 1, 1) for p in parts]
-        return [jnp.where(lane == 0, rolled[h], rolled[h + 1]) for h in halves]
-
-    def columns(parts):
-        ahead = shift_left(parts)
-        tiles = []
-        for h in halves:
-            swapped = pltpu.roll(ahead[h], 4, 0)
-            even = jnp.where(low_half, parts[h], swapped)
-            odd = jnp.where(low_half, swapped, parts[h])
-            high0 = even.astype(bf16).astype(f32)
-            high1 = odd.astype(bf16).astype(f32)
-            tiles.append(
-                (
-                    jnp.concatenate([high0, even - high0], 0).astype(bf16),
-                    jnp.concatenate([high0, high1], 0).astype(bf16),
-                    jnp.concatenate([high1, odd - high1], 0).astype(bf16),
-                )
-            )
-        return tiles
-
-    def put_columns(buffers, z, p, parts):
-        for h, tiles in enumerate(columns(parts)):
-            for j in range(3):
-                for b in buffers:
-                    KB[b, z, p, 16 * j : 16 * j + 16, h * LANES : (h + 1) * LANES] = tiles[j]
-
+    sides = plan.sides()
     mid = slice(R, R + 4 * Y)
     for z in range(Z):
         U[offset + z, :, mid, :] = xv[z, :, : 4 * Y, :]
@@ -293,8 +316,7 @@
             U[at_u + i, :, mid, :] = zrecv[i]
         for i in range(T - 1):
             V[at_v + i, :, mid, :] = zrecv[T + i]
-    U[ZB:, :, :, :] = jnp.zeros((ZS - ZB, H, 4 * YB, LANES), f32)
-    V[ZB:, :, :, :] = jnp.zeros((ZS - ZB, H, 4 * YB, LANES), f32)
+        V[lacks, :, :, :] = jnp.zeros((H, 4 * YB, LANES), f32)
     for s in range(T):
         G[s] = jnp.zeros((H, 4 * YB, LANES), f32)
         G[s, :, mid, :] = gown[s]
@@ -308,6 +330,42 @@
         for t, (s, h, k, n_pairs) in enumerate(waves):
             at = aligned(jnp.where(from_next, R + 4 * Y, R - 8 * n_pairs) + 8 * k)
             G[s, h, pl.ds(at, 8), :] = source[len(own) + t]
+
+    def own_layer(z, carry):
+        rows = [*range(0, YB - 7, 8), YB - 8]
+        prepare(plan, tables, U, V, DM, lam, mu, columns, offset + z, range(PB), sorted(set(rows)))
+        columns[offset + z, PB] = jnp.zeros((48, X), bf16)
+        return carry
+
+    lax.fori_loop(0, Z, own_layer, 0)
+    for at_u, at_v, lacks in halo_places(plan, scal):
+
+        def halo_layer(i, carry):
+            rows = range(plan.hy, plan.hy + Y, 8)
+            prepare(plan, tables, U, V, DM, lam, mu, columns, at_u + i, range(P0, P0 + Y // 2), rows)
+            columns[at_u + i, PB] = jnp.zeros((48, X), bf16)
+            return carry
+
+        lax.fori_loop(0, T, halo_layer, 0)
+    for z in range(ZB, ZS):
+        for ref in (U, V, DM, lam, mu, columns):
+            ref[z] = jnp.zeros(ref.shape[1:], ref.dtype)
+
+
+def main_kernel(plan, tables, weights, *refs):
+    corners = refs[: len(refs) - 18]
+    G = refs[len(refs) - 13]
+    out_u, out_v, U, V, DM, lam, mu, columns, CI, F, spare_columns = refs[len(refs) - 11 :]
+    Z, Y, X, H, T = plan.Z, plan.Y, plan.X, plan.H, plan.T
+    PB, P0, R, ZB, ZS, YB = plan.PB, plan.P0, plan.hrow, plan.ZB, plan.ZS, plan.YB
+    scal = place(plan)
+    offset = scal[1]
+    sides = plan.sides()
+    halves = range(H)
+    n_levels = tables.shape[0] // 2
+    low_half = first_half()
+    zero = jnp.zeros((8, LANES), f32)
+
     tiles = plan.corner_tiles()
     for k, (at_u, at_v, lacks) in enumerate(halo_places(plan, scal)):
         for source, from_next in zip(corners, sides):
@@ -319,51 +377,17 @@
                     V[at_v + i - T, h, pl.ds(row, 8), :] = tile
 
             take_halo(plan, tiles, source, k * len(tiles), from_next, write)
-        V[lacks, :, :, :] = jnp.zeros((H, 4 * YB, LANES), f32)
-
-    n_levels = tables.shape[0] // 2
-
-    def prepare(z, carry):
-        for h in halves:
-            for y in range(0, plan.YL, 8):
-                count = min(8, YB - y)
-                if count == 8:
-                    level = U[z, h, pl.ds(4 * y + 3, 8, stride=4), :]
-                    first = y
-                else:
-                    first = YB - 8
-                    level = U[z, h, pl.ds(4 * first + 3, 8, stride=4), :]
-                dil = jnp.zeros((8, LANES), f32)
-                she = jnp.zeros((8, LANES), f32)
-                for k in range(n_levels):
-                    here = level == float(k + 1)
-                    dil = jnp.where(here, tables[k], dil)
-                    she = jnp.where(here, tables[n_levels + k], she)
-                lam[z, h, first : first + 8, :] = dil
-                mu[z, h, first : first + 8, :] = she
-        for p in range(PB):
-            at = slice(8 * p, 8 * p + 8)
-            for h in halves:
-                v = V[z, h, at, :]
-                mass = jnp.where(
-                    low_half,
-                    jnp.broadcast_to(v[3:4, :], (8, LANES)),
-                    jnp.broadcast_to(v[7:8, :], (8, LANES)),
-                )
-                DM[z, h, at, :] = jnp.where(spare, 0.0, time_step * mass)
-            put_columns((0,), z, p, [U[z, h, at, :] for h in halves])
-        for b in range(2):
-            for p in range(widest_pair + 1 if b else PB, PB + 1):
-                KB[b, z, p] = jnp.zeros((48, X), bf16)
-        return carry
-
+
+        def halo_layer(i, carry):
+            pairs = [*range(P0), *range(P0 + Y // 2, PB)]
+            prepare(plan, tables, U, V, DM, lam, mu, columns, at_u + i, pairs, (0, YB - 8))
+            return carry
+
+        lax.fori_loop(0, T, halo_layer, 0)
     widest_pair = (plan.hy + Y + T - 2) // 2
-    lax.fori_loop(0, ZB, prepare, 0)
-    for z in range(ZB, ZS):
-        for b in range(2):
-            KB[b, z] = jnp.zeros((PB + 1, 48, X), bf16)
-        for ref in (DM, lam, mu):
-            ref[z] = jnp.zeros(ref.shape[1:], f32)
+    for z in range(ZS):
+        for p in range(widest_pair + 1 if z < ZB else 0, PB + 1):
+            spare_columns[z, p] = jnp.zeros((48, X), bf16)
 
     bottom = offset + Z - 1
     wave = tables[2 * n_levels]
@@ -375,7 +399,7 @@
 
     def one_step(s, final):
         d = T - 1 - s
-        cur, new = s % 2, 1 - s % 2
+        cur, new = (columns, spare_columns)[:: 1 - 2 * (s % 2)]
         p_first = (plan.hy - d - 1) // 2
         p_last = (plan.hy + Y - 1 + d) // 2
         if plan.D == 1:
@@ -401,7 +425,7 @@
             other = [
                 pltpu.roll(jnp.where(low_half, g1[h], g0[h]), 4, 0) for h in halves
             ]
-            other = shift_right(other)
+            other = shift_right(plan, other)
             fresh = []
             for h in halves:
                 force = jnp.where(low_half, g0[h], g1[h]) + other[h]
@@ -411,7 +435,7 @@
                 U[z, h, at, :] = u
                 fresh.append(u)
             if not final:
-                put_columns((new,), z, p, fresh)
+                put_columns(plan, new, z, p, fresh)
 
         def two_layers(i, carry):
             z0 = p_z0 + 2 * i
@@ -419,12 +443,12 @@
             for p in range(p_first, p_last + 1):
                 right = jnp.concatenate(
                     [
-                        KB[cur, z0, p],
-                        KB[cur, z0, p + 1, :32],
-                        KB[cur, z0 + 1, p],
-                        KB[cur, z0 + 1, p + 1, :32],
-                        KB[cur, z0 + 2, p],
-                        KB[cur, z0 + 2, p + 1],
+                        cur[z0, p],
+                        cur[z0, p + 1, :32],
+                        cur[z0 + 1, p],
+                        cur[z0 + 1, p + 1, :32],
+                        cur[z0 + 2, p],
+                        cur[z0 + 2, p + 1, :32],
                     ],
                     0,
                 )
@@ -503,18 +527,23 @@
     n_tables = 2 * dilation_table.shape[0] + 1
     weights, tables = pl.pallas_call(
         matrix_kernel,
-        out_shape=[pltpu.VMEM((256, 256), bf16), pltpu.VMEM((n_tables, 8, LANES), f32)],
+        out_shape=[pltpu.VMEM((256, 240), bf16), pltpu.VMEM((n_tables, 8, LANES), f32)],
         in_specs=[vmem()] * 3 + [smem()] * 3,
         out_specs=[vmem()] * 2,
         compiler_params=room,
         name="matrix",
     )(
-        stiffness_pair.reshape(48, 24),
-        jnp.asarray(rows, bf16),
-        jnp.asarray(cols, bf16),
-        dilation_table,
-        shear_table,
-        impedance,
+        *[
+            pltpu.with_memory_space_constraint(a, pltpu.HBM)
+            for a in (
+                stiffness_pair.reshape(48, 24),
+                jnp.asarray(rows, bf16),
+                jnp.asarray(cols, bf16),
+                dilation_table,
+                shear_table,
+                impedance,
+            )
+        ]
     )
 
     n_sends = 0 if D == 1 else 1 if plan.swap else 2
@@ -560,28 +589,35 @@
         )(*[pltpu.with_memory_space_constraint(a, pltpu.VMEM) for a in zrecvs])
         corners = [trade(corner_first, 1), trade(corner_second, 0)]
     near = lambda arrays: [pltpu.with_memory_space_constraint(a, pltpu.VMEM) for a in arrays]
-    zrecvs, corners = near(zrecvs), near(corners)
-    first, second, xv, g, weights, tables = near([*firsts, xv, g, weights, tables])
     grid = (plan.ZS, H, 4 * plan.YB, LANES)
-    new_u, new_v = pl.pallas_call(
+    moduli = (plan.ZS, H, plan.YB, LANES)
+    held = (plan.ZS, plan.PB + 1, 48, X)
+    state = [local(*grid), local(*grid), local(*grid), local(*moduli), local(*moduli)]
+    columns = pltpu.VMEM(held, bf16)
+    begun = pl.pallas_call(
+        lambda *refs: begin_kernel(plan, *refs),
+        out_shape=[*state, local(T, H, 4 * plan.YB, LANES), columns],
+        in_specs=[vmem()] * (5 + len(zrecvs)),
+        out_specs=[vmem()] * 7,
+        compiler_params=room,
+        name="begin",
+    )(*near([tables, xv, g, *zrecvs, *firsts]))
+    *state_in, waves_in, columns_in = near(begun)
+    n = 2 + len(corners)
+    new_u, new_v, *_ = pl.pallas_call(
         lambda *refs: main_kernel(plan, *refs),
-        out_shape=[shape(3, Z, Y, X)] * 2,
-        in_specs=[vmem()] * (6 + len(zrecvs) + len(corners)),
-        out_specs=[vmem()] * 2,
+        out_shape=[shape(3, Z, Y, X), shape(3, Z, Y, X), *state, columns],
+        in_specs=[vmem()] * (n + 7),
+        out_specs=[vmem()] * 8,
+        input_output_aliases={n + i: 2 + i for i in range(5)} | {n + 6: 7},
         scratch_shapes=[
-            pltpu.VMEM(grid, f32),
-            pltpu.VMEM(grid, f32),
-            pltpu.VMEM(grid, f32),
-            pltpu.VMEM((plan.ZS, H, plan.YL, LANES), f32),
-            pltpu.VMEM((plan.ZS, H, plan.YL, LANES), f32),
-            pltpu.VMEM((T, H, 4 * plan.YB, LANES), f32),
             pltpu.VMEM((H, 4 * plan.YB, LANES), f32),
             pltpu.VMEM((plan.PB, 2, H, 8, LANES), f32),
-            pltpu.VMEM((2, plan.ZS, plan.PB + 1, 48, X), bf16),
+            pltpu.VMEM(held, bf16),
         ],
         compiler_params=room,
         name="steps",
-    )(tables, weights, xv, g, *zrecvs, first, second, *corners)
+    )(*near([tables, weights, *corners]), *state_in, waves_in, columns_in)
     return new_u, new_v
 
 

time: 38 us -> 37.3 us (0.982)
  Pallas kernels: 17 us -> 18.5 us
  waiting for transfers between devices: 8.72 us -> 7.23 us
  local copies, waits for them, and re-layouts: 0.58 us -> 0 us
    pallas_call x1 -> x2, Pallas kernels: 1.01 us -> 3.14 us  [the longest x1 1.71 us: per_device(): pl.pallas_call(lambda *refs: begin_kernel(plan, *refs), out_shape=[*state...]
    ppermute x4, waiting for transfers between devices: 4.71 us -> 3.19 us  [trade(): return lax.ppermute(array, 'lat', pairs + [(j, i) for i, j in pairs])]
    pallas_call x1, Pallas kernels: 14.6 us -> 14 us  [per_device(): pl.pallas_call(lambda *refs: main_kernel(plan, *refs), out_shape=[shape(3...]
    unnamed x12 -> x0, local copies, waits for them, and re-layouts: 0.58 us -> none
  transfers between devices with their start and end apart: 5 -> 5, of which waited for: 3 -> 3; matrix products, arithmetic and copies ran while one was open for 0% -> 0% of each run, Pallas kernels for 3% -> 9%
where the time goes in v4:
time: 37.3 us; the launch traced here: 37.2 us
  Pallas kernels  18.5 us (50%)
  starting transfers between devices  10.8 us (29%)
  waiting for transfers between devices  7.23 us (19%)
  between operations  0.69 us (2%)
    pallas_call x1, Pallas kernels, per_device(): pl.pallas_call(lambda *refs: main_kernel(plan, *refs), out_shape=[shape(3...  14 us
    ppermute x4, starting transfers between devices, trade(): return lax.ppermute(array, 'lat', pairs + [(j, i) for i, j in pairs])  8.66 us
    ppermute x1, waiting for transfers between devices, per_device(): zrecvs = [lax.ppermute(sends[0], 'depth', [(0, 1), (1, 0)])]  4.05 us
    ppermute x4, waiting for transfers between devices, trade(): return lax.ppermute(array, 'lat', pairs + [(j, i) for i, j in pairs])  3.19 us
    ppermute x1, starting transfers between devices, per_device(): zrecvs = [lax.ppermute(sends[0], 'depth', [(0, 1), (1, 0)])]  2.09 us
    pallas_call x1, Pallas kernels, per_device(): pl.pallas_call(lambda *refs: begin_kernel(plan, *refs), out_shape=[*state...  1.71 us
    pallas_call x1, Pallas kernels, per_device(): pl.pallas_call(matrix_kernel, out_shape=[pltpu.VMEM((256, 240), bf16), pl...  1.43 us
    pallas_call x1, Pallas kernels, per_device(): pl.pallas_call(lambda *refs: pack_kernel(plan, *refs), out_shape=[local(Z...  1.33 us
  transfers between devices with their start and end apart: 5, of which 3 were waited for; matrix products, arithmetic and copies ran while one was open for 0% of the time, Pallas kernels for 9%

profile of v4, /device:TPU:1, one launch (start us, length us, event | category | flops | bytes accessed | tf_op | source)
XLA Modules:
  0.0 37.2 jit_solution(3692233316464247506)
XLA Ops:
  0.6 1.3 %pack.1 = (f32[8,2,64,128]{3,2,1,0:T(8,128)S(1)}, f32[6,2,32,128]{3,2,1,0:T(8,128)S(1)}, f32[106,8,128]{2,1,0:T(8,128)S(1)}, f32[106,8,128]{2,1,0:T(8,128)S(1)}, f32[11,2,32,128]{3,2,1,0:T(8,128)S(1)}) custom-call(f32[3,8,8,256]{3,2,1,0:T(8,128)} %refs_0_.1, f32[3,8,8,256]{3,2,1,0:T(8,128)} %refs_1_.1, f32[8,8,256]{2,1,0:T(8,128)} %refs_2_.1, ...), custom_call_target="tpu_custom_call" | custom-call | tf_op jit(solution)/shard_map/pack/pallas_call | solution.py:553
  2.0 2.1 %collective-permute-start = (f32[11,2,32,128]{3,2,1,0:T(8,128)S(1)}, f32[11,2,32,128]{3,2,1,0:T(8,128)S(1)}, u32[]{:S(2)}, u32[]{:S(2)}) collective-permute-start(f32[11,2,32,128]{3,2,1,0:T(8,128)S(1)} %get-tuple-element.22), channel_id=1, source_target_pairs={{0,16},{16,0},{1,17},{17,1},{2,18},{18,2},{3,19},{19,3},{4,20},{20... | collective-permute-start | bytes 1081352 | tf_op jit(solution)/shard_map/ppermute | solution.py:572
  4.1 4.0 %collective-permute-start.3 = (f32[106,8,128]{2,1,0:T(8,128)S(1)}, f32[106,8,128]{2,1,0:T(8,128)S(1)}, u32[]{:S(2)}, u32[]{:S(2)}) collective-permute-start(f32[106,8,128]{2,1,0:T(8,128)S(1)} %get-tuple-element.27), channel_id=1, source_target_pairs={{1,2},{3,4},{5,6},{7,8},{9,10},{11,12},{13,14},{2,1},{4,3},{6,5},{... | collective-permute-start | bytes 1302536 | tf_op jit(solution)/shard_map/ppermute | solution.py:567
  8.1 0.1 collective-permute-start.4
  8.1 4.0 %collective-permute-done.refs_0_.refs_3_ = f32[11,2,32,128]{3,2,1,0:T(8,128)S(1)} collective-permute-done((f32[11,2,32,128]{3,2,1,0:T(8,128)S(1)}, f32[11,2,32,128]{3,2,1,0:T(8,128)S(1)}, u32[]{:S(2)}, u32[]{:S(2)}) %collective-permute-start) | collective-permute-done | bytes 360480 | tf_op jit(solution)/shard_map/ppermute | solution.py:572
  12.2 4.5 %collective-permute-start.1 = (f32[61,8,128]{2,1,0:T(8,128)S(1)}, f32[61,8,128]{2,1,0:T(8,128)S(1)}, u32[]{:S(2)}, u32[]{:S(2)}) collective-permute-start(f32[61,8,128]{2,1,0:T(8,128)S(1)} %get-tuple-element.23), channel_id=1, source_target_pairs={{1,2},{3,4},{5,6},{7,8},{9,10},{11,12},{13,14},{2,1},{4,3},{6,5},{... | collective-permute-start | bytes 749576 | tf_op jit(solution)/shard_map/ppermute | solution.py:567
  16.8 0.1 collective-permute-start.2
  16.9 1.4 %matrix.1 = (bf16[256,240]{1,0:T(8,128)(2,1)S(1)}, f32[17,8,128]{2,1,0:T(8,128)S(1)}) custom-call(f32[48,24]{1,0:T(8,128)} %bitcast.1, bf16[4,64,48]{2,1,0:T(8,128)(2,1)} %constant.4.clone.rows_ref, bf16[2,4,24,240]{3,2,1,0:T(8,128)(2,1)} %constant.5.clone.cols_ref, f32[8]{0:T(128)} %dilations.1, f32[8]{0:T(128)} %shears.1, f32[3]{0:T(128)} %imp.1), custom_call_target="tpu_custom_call" | custom-call | tf_op jit(solution)/shard_map/matrix/pallas_call | solution.py:528
  18.3 2.2 %collective-permute-done.3.refs_4_ = f32[106,8,128]{2,1,0:T(8,128)S(1)} collective-permute-done((f32[106,8,128]{2,1,0:T(8,128)S(1)}, f32[106,8,128]{2,1,0:T(8,128)S(1)}, u32[]{:S(2)}, u32[]{:S(2)}) %collective-permute-start.3) | collective-permute-done | bytes 434208 | tf_op jit(solution)/shard_map/ppermute | solution.py:567
  20.5 0.0 collective-permute-done.4.refs_5_
  20.5 1.7 %begin.1 = (f32[16,2,80,128]{3,2,1,0:T(8,128)S(1)}, f32[16,2,80,128]{3,2,1,0:T(8,128)S(1)}, f32[16,2,80,128]{3,2,1,0:T(8,128)S(1)}, f32[16,2,20,128]{3,2,1,0:T(8...) custom-call(f32[17,8,128]{2,1,0:T(8,128)S(1)} %get-tuple-element.20., ...), custom_call_target="tpu_custom_call" | custom-call | tf_op jit(solution)/shard_map/begin/pallas_call | solution.py:597
  22.2 1.0 %collective-permute-done.1.refs_2_ = f32[61,8,128]{2,1,0:T(8,128)S(1)} collective-permute-done((f32[61,8,128]{2,1,0:T(8,128)S(1)}, f32[61,8,128]{2,1,0:T(8,128)S(1)}, u32[]{:S(2)}, u32[]{:S(2)}) %collective-permute-start.1) | collective-permute-done | bytes 249888 | tf_op jit(solution)/shard_map/ppermute | solution.py:567
  23.2 0.0 collective-permute-done.2.refs_3_
  23.2 14.0 %steps.1 = (f32[3,8,8,256]{3,2,1,0:T(8,128)}, f32[3,8,8,256]{3,2,1,0:T(8,128)}, f32[16,2,80,128]{3,2,1,0:T(8,128)S(1)}, f32[16,2,80,128]{3,2,1,0:T(8,128)S(1)}, ...) custom-call(f32[17,8,128]{2,1,0:T(8,128)S(1)} %get-tuple-element.20., ...), custom_call_target="tpu_custom_call", output_to_operand_aliasing={{2}: (4, {}), {3}: (5, {}), {4}: (6, {}), {5}: (7, {}), {6}... | custom-call | tf_op jit(solution)/shard_map/steps/pallas_call | solution.py:607
  (1 shorter events, 0.0 us)
Async XLA Ops:
  2.0 10.2 %collective-permute-start = (f32[11,2,32,128]{3,2,1,0:T(8,128)S(1)}, f32[11,2,32,128]{3,2,1,0:T(8,128)S(1)}, u32[]{:S(2)}, u32[]{:S(2)}) collective-permute-start(f32[11,2,32,128]{3,2,1,0:T(8,128)S(1)} %get-tuple-element.22), channel_id=1, source_target_pairs={{0,16},{16,0},{1,17},{17,1},{2,18},{18,2},{3,19},{19,3},{4,20},{20... | collective-permute-start | bytes 1081352 | tf_op jit(solution)/shard_map/ppermute | solution.py:572
  4.1 16.5 %collective-permute-start.3 = (f32[106,8,128]{2,1,0:T(8,128)S(1)}, f32[106,8,128]{2,1,0:T(8,128)S(1)}, u32[]{:S(2)}, u32[]{:S(2)}) collective-permute-start(f32[106,8,128]{2,1,0:T(8,128)S(1)} %get-tuple-element.27), channel_id=1, source_target_pairs={{1,2},{3,4},{5,6},{7,8},{9,10},{11,12},{13,14},{2,1},{4,3},{6,5},{... | collective-permute-start | bytes 1302536 | tf_op jit(solution)/shard_map/ppermute | solution.py:567
  8.1 12.5 %collective-permute-start.4 = (f32[106,8,128]{2,1,0:T(8,128)S(1)}, f32[106,8,128]{2,1,0:T(8,128)S(1)}, u32[]{:S(2)}, u32[]{:S(2)}) collective-permute-start(f32[106,8,128]{2,1,0:T(8,128)S(1)} %get-tuple-element.28), channel_id=1, source_target_pairs={{0,1},{2,3},{4,5},{6,7},{8,9},{10,11},{12,13},{14,15},{1,0},{3,2},... | collective-permute-start | bytes 1302536 | tf_op jit(solution)/shard_map/ppermute | solution.py:567
  12.2 11.0 %collective-permute-start.1 = (f32[61,8,128]{2,1,0:T(8,128)S(1)}, f32[61,8,128]{2,1,0:T(8,128)S(1)}, u32[]{:S(2)}, u32[]{:S(2)}) collective-permute-start(f32[61,8,128]{2,1,0:T(8,128)S(1)} %get-tuple-element.23), channel_id=1, source_target_pairs={{1,2},{3,4},{5,6},{7,8},{9,10},{11,12},{13,14},{2,1},{4,3},{6,5},{... | collective-permute-start | bytes 749576 | tf_op jit(solution)/shard_map/ppermute | solution.py:567
  16.8 6.4 %collective-permute-start.2 = (f32[61,8,128]{2,1,0:T(8,128)S(1)}, f32[61,8,128]{2,1,0:T(8,128)S(1)}, u32[]{:S(2)}, u32[]{:S(2)}) collective-permute-start(f32[61,8,128]{2,1,0:T(8,128)S(1)} %get-tuple-element.24), channel_id=1, source_target_pairs={{0,1},{2,3},{4,5},{6,7},{8,9},{10,11},{12,13},{14,15},{1,0},{3,2},... | collective-permute-start | bytes 749576 | tf_op jit(solution)/shard_map/ppermute | solution.py:567

commit v5 on v4

--- a/solution.py
+++ b/solution.py
@@ -104,7 +104,6 @@
 
 def selectors():
     rows = np.zeros((4, 64, 48), np.float32)
-    cols = np.zeros((2, 4, 24, 240), np.float32)
 
     def half(parity, dx):
         return 4 * (dx ^ parity)
@@ -112,7 +111,6 @@
     blocks = [(0, 0, 0), (8, 0, 0), (16, 0, 1), (24, 1, 1), (32, 1, 0), (40, 1, 0), (48, 2, 0), (56, 2, 0), (64, 2, 1)]
     for ez in range(2):
         for ey in range(2):
-            e = 2 * ez + ey
             for lm in range(2):
                 for dz in range(2):
                     for dy in range(2):
@@ -120,29 +118,46 @@
                             for c in range(3):
                                 dof = (4 * dz + 2 * dy + dx) * 3 + c
                                 r = half((ey + dy) % 2, dx) + c
-                                rows[e, ((lm * 2 + dz) * 2 + dy) * 8 + r, lm * 24 + dof] = 1
+                                rows[2 * ez + ey, ((lm * 2 + dz) * 2 + dy) * 8 + r, lm * 24 + dof] = 1
+    cols = []
+    for layers, eys, (start, stop) in VARIANTS:
+        width = stop - start
+        elements = [(ez, ey) for ez in range(layers) for ey in eys]
+        part = np.zeros((2, len(elements), 24, (layers + 1) * width), np.float32)
+        for e, (ez, ey) in enumerate(elements):
             for base, node, low in blocks:
-                for zn in range(3):
+                for zn in range(layers + 1):
                     dz, dy = zn - ez, node - ey
                     if dz in (0, 1) and dy in (0, 1):
+                        assert start <= base < stop
                         for dx in range(2):
                             for c in range(3):
                                 dof = (4 * dz + 2 * dy + dx) * 3 + c
-                                cols[low, e, dof, zn * 80 + base + half(node % 2, dx) + c] = 1
+                                part[low, e, dof, zn * width + base - start + half(node % 2, dx) + c] = 1
+        cols.append(part)
     return rows, cols
 
 
-def matrix_kernel(stiff_ref, rows_ref, cols_ref, dilations, shears, imp, out_ref, tiles_ref):
+VARIANTS = [(n, eys, span) for n in (2, 1) for eys, span in (((0, 1), (0, 80)), ((0,), (0, 48)), ((1,), (16, 80)))]
+
+
+def matrix_kernel(stiff_ref, rows_ref, dilations, shears, imp, *refs):
+    cols_refs, out_refs, tiles_ref = refs[: len(VARIANTS)], refs[len(VARIANTS) : -1], refs[-1]
     stiff = stiff_ref[...]
     high = stiff.astype(bf16)
     low = (stiff - high.astype(f32)).astype(bf16)
-    for e in range(4):
-        total = None
-        for part, k in ((high, 0), (low, 1)):
-            picked = jnp.dot(rows_ref[e], part, preferred_element_type=f32).astype(bf16)
-            placed = jnp.dot(picked, cols_ref[k, e], preferred_element_type=f32)
-            total = placed if total is None else total + placed
-        out_ref[64 * e : 64 * e + 64, :] = total.astype(bf16)
+    picked = [
+        [jnp.dot(rows_ref[e], part, preferred_element_type=f32).astype(bf16) for part in (high, low)]
+        for e in range(4)
+    ]
+    for (layers, eys, _), cols_ref, out_ref in zip(VARIANTS, cols_refs, out_refs):
+        elements = [2 * ez + ey for ez in range(layers) for ey in eys]
+        for i, e in enumerate(elements):
+            total = None
+            for k in range(2):
+                placed = jnp.dot(picked[e][k], cols_ref[k, i], preferred_element_type=f32)
+                total = placed if total is None else total + placed
+            out_ref[64 * i : 64 * i + 64, :] = total.astype(bf16)
     n = dilations.shape[0]
     for k in range(n):
         tiles_ref[k] = jnp.full((8, LANES), dilations[k], f32)
@@ -352,8 +367,9 @@
             ref[z] = jnp.zeros(ref.shape[1:], ref.dtype)
 
 
-def main_kernel(plan, tables, weights, *refs):
-    corners = refs[: len(refs) - 18]
+def main_kernel(plan, tables, *refs):
+    weights = refs[: len(VARIANTS)]
+    corners = refs[len(VARIANTS) : len(refs) - 18]
     G = refs[len(refs) - 13]
     out_u, out_v, U, V, DM, lam, mu, columns, CI, F, spare_columns = refs[len(refs) - 11 :]
     Z, Y, X, H, T = plan.Z, plan.Y, plan.X, plan.H, plan.T
@@ -400,17 +416,16 @@
     def one_step(s, final):
         d = T - 1 - s
         cur, new = (columns, spare_columns)[:: 1 - 2 * (s % 2)]
-        p_first = (plan.hy - d - 1) // 2
-        p_last = (plan.hy + Y - 1 + d) // 2
+        e_first, e_last = plan.hy - d - 1, plan.hy + Y - 1 + d
+        p_first, p_last = e_first // 2, e_last // 2
         if plan.D == 1:
-            p_z0, count = 0, -(-Z // 2)
+            first_z, n_z = 0, Z
         elif plan.swap:
-            top = scal[0] == 0
-            count = -(-(Z + d + 1) // 2)
-            p_z0 = jnp.where(top, 0, ZB - 2 * count)
+            n_z = Z + d + 1
+            first_z = jnp.where(scal[0] == 0, 0, ZB - n_z)
         else:
-            p_z0 = T - d - 1
-            count = -(-(Z + 2 * d + 1) // 2)
+            first_z, n_z = T - d - 1, Z + 2 * d + 1
+        single, count = n_z % 2, n_z // 2
 
         for p in range(p_first, p_last + 1):
             at = slice(8 * p, 8 * p + 8)
@@ -437,31 +452,28 @@
             if not final:
                 put_columns(plan, new, z, p, fresh)
 
-        def two_layers(i, carry):
-            z0 = p_z0 + 2 * i
-            side = [[zero for _ in halves] for _ in range(3)]
+        def layer_row(z0, n_layers):
+            side = [[zero for _ in halves] for _ in range(n_layers + 1)]
             for p in range(p_first, p_last + 1):
-                right = jnp.concatenate(
-                    [
-                        cur[z0, p],
-                        cur[z0, p + 1, :32],
-                        cur[z0 + 1, p],
-                        cur[z0 + 1, p + 1, :32],
-                        cur[z0 + 2, p],
-                        cur[z0 + 2, p + 1, :32],
-                    ],
-                    0,
-                )
-                product = jnp.dot(weights[...], right, preferred_element_type=f32)
-                node = [[None] * 3 for _ in range(3)]
-                for zn in range(3):
-                    node[zn][0] = side[zn]
+                eys = tuple(ey for ey in range(2) if e_first <= 2 * p + ey <= e_last)
+                kind = [(n, e) for n, e, _ in VARIANTS].index((n_layers, eys))
+                pieces = []
+                for zn in range(n_layers + 1):
+                    start, stop = VARIANTS[kind][2]
+                    pieces.append(cur[z0 + zn, p, start:48])
+                    if stop > 48:
+                        pieces.append(cur[z0 + zn, p + 1, : stop - 48])
+                right = jnp.concatenate(pieces, 0)
+                product = jnp.dot(weights[kind][...], right, preferred_element_type=f32)
+                node = [[None] * 3 for _ in range(n_layers + 1)]
+                for zn in range(n_layers + 1):
+                    node[zn][0] = list(side[zn])
                 for y in range(2):
                     above = [F[p, y, h] for h in halves]
                     node[0][y] = above if y else [a + b for a, b in zip(node[0][0], above)]
-                for ez in range(2):
-                    for ey in range(2):
-                        base = 64 * (2 * ez + ey)
+                for ez in range(n_layers):
+                    for j, ey in enumerate(eys):
+                        base = 64 * (len(eys) * ez + j)
                         y = 2 * p + ey
                         for h in halves:
                             lanes = slice(h * LANES, (h + 1) * LANES)
@@ -477,25 +489,30 @@
                                     slot = node[ez + dz][ey + dy]
                                     if slot is None:
                                         slot = node[ez + dz][ey + dy] = [None] * H
-                                    elif slot is side[ez + dz]:
-                                        slot = node[ez + dz][ey + dy] = list(slot)
                                     slot[h] = part if slot[h] is None else slot[h] + part
                 for y in range(2):
                     for h in halves:
-                        F[p, y, h] = node[2][y][h]
-                finish(z0, p, node[0][0], node[0][1])
-                finish(z0 + 1, p, node[1][0], node[1][1])
-                side = [node[zn][2] for zn in range(3)]
+                        F[p, y, h] = node[n_layers][y][h]
+                for zn in range(n_layers):
+                    finish(z0 + zn, p, node[zn][0], node[zn][1])
+                side = [node[zn][2] or [zero for _ in halves] for zn in range(n_layers + 1)]
+
+        def rows(first, number, carry):
+            for i in range(number):
+                layer_row(first_z + single + 2 * (first + i), 2)
             return carry
 
-        def chunk(first, rows):
-            for i in range(rows):
-                two_layers(first + i, 0)
-
-        straight = count if plan.ZB <= 16 else 1
-        full, rest = count // straight, count % straight
-        lax.fori_loop(0, full * scal[3], lambda i, c: (chunk(straight * i, straight), c)[1], 0)
-        assert rest == 0
+        def whole_step(i, carry):
+            if single:
+                layer_row(first_z, 1)
+            return rows(0, count, carry)
+
+        if plan.ZB <= 16:
+            lax.fori_loop(0, scal[3], whole_step, 0)
+        else:
+            if single:
+                layer_row(first_z, 1)
+            lax.fori_loop(0, count, lambda i, c: rows(i, 1, c), 0)
 
     for s in range(T):
         one_step(s, s == T - 1)
@@ -525,11 +542,12 @@
     room = pltpu.CompilerParams(vmem_limit_bytes=40 * 2**20)
     rows, cols = selectors()
     n_tables = 2 * dilation_table.shape[0] + 1
-    weights, tables = pl.pallas_call(
+    made = pl.pallas_call(
         matrix_kernel,
-        out_shape=[pltpu.VMEM((256, 240), bf16), pltpu.VMEM((n_tables, 8, LANES), f32)],
-        in_specs=[vmem()] * 3 + [smem()] * 3,
-        out_specs=[vmem()] * 2,
+        out_shape=[pltpu.VMEM((64 * part.shape[1], part.shape[3]), bf16) for part in cols]
+        + [pltpu.VMEM((n_tables, 8, LANES), f32)],
+        in_specs=[vmem()] * 2 + [smem()] * 3 + [vmem()] * len(cols),
+        out_specs=[vmem()] * (len(cols) + 1),
         compiler_params=room,
         name="matrix",
     )(
@@ -538,13 +556,14 @@
             for a in (
                 stiffness_pair.reshape(48, 24),
                 jnp.asarray(rows, bf16),
-                jnp.asarray(cols, bf16),
                 dilation_table,
                 shear_table,
                 impedance,
+                *[jnp.asarray(part, bf16) for part in cols],
             )
         ]
     )
+    weights, tables = made[:-1], made[-1]
 
     n_sends = 0 if D == 1 else 1 if plan.swap else 2
     tiles, waves = plan.own_tiles()
@@ -603,7 +622,7 @@
         name="begin",
     )(*near([tables, xv, g, *zrecvs, *firsts]))
     *state_in, waves_in, columns_in = near(begun)
-    n = 2 + len(corners)
+    n = 1 + len(weights) + len(corners)
     new_u, new_v, *_ = pl.pallas_call(
         lambda *refs: main_kernel(plan, *refs),
         out_shape=[shape(3, Z, Y, X), shape(3, Z, Y, X), *state, columns],
@@ -617,7 +636,7 @@
         ],
         compiler_params=room,
         name="steps",
-    )(*near([tables, weights, *corners]), *state_in, waves_in, columns_in)
+    )(*near([tables, *weights, *corners]), *state_in, waves_in, columns_in)
     return new_u, new_v
 
 

time: 37.3 us -> 36.4 us (0.976)
  Pallas kernels: 18.5 us -> 17.6 us
    pallas_call x1, Pallas kernels: 14 us -> 13 us  [per_device(): pl.pallas_call(lambda *refs: main_kernel(plan, *refs), out_shape=[shape(3...]
where the time goes in v5:
time: 36.4 us; the launch traced here: 36.2 us
  Pallas kernels  17.6 us (48%)
  starting transfers between devices  10.8 us (30%)
  waiting for transfers between devices  7.17 us (20%)
  between operations  0.69 us (2%)
    pallas_call x1, Pallas kernels, per_device(): pl.pallas_call(lambda *refs: main_kernel(plan, *refs), out_shape=[shape(3...  13 us
    ppermute x4, starting transfers between devices, trade(): return lax.ppermute(array, 'lat', pairs + [(j, i) for i, j in pairs])  8.66 us
    ppermute x1, waiting for transfers between devices, per_device(): zrecvs = [lax.ppermute(sends[0], 'depth', [(0, 1), (1, 0)])]  4.05 us
    ppermute x4, waiting for transfers between devices, trade(): return lax.ppermute(array, 'lat', pairs + [(j, i) for i, j in pairs])  3.13 us
    ppermute x1, starting transfers between devices, per_device(): zrecvs = [lax.ppermute(sends[0], 'depth', [(0, 1), (1, 0)])]  2.09 us
    pallas_call x1, Pallas kernels, per_device(): pl.pallas_call(lambda *refs: begin_kernel(plan, *refs), out_shape=[*state...  1.71 us
    pallas_call x1, Pallas kernels, per_device(): pl.pallas_call(matrix_kernel, out_shape=[pltpu.VMEM((64 * part.shape[1],...  1.49 us
    pallas_call x1, Pallas kernels, per_device(): pl.pallas_call(lambda *refs: pack_kernel(plan, *refs), out_shape=[local(Z...  1.33 us
  transfers between devices with their start and end apart: 5, of which 3 were waited for; matrix products, arithmetic and copies ran while one was open for 0% of the time, Pallas kernels for 9%

profile of v5, /device:TPU:1, one launch (start us, length us, event | category | flops | bytes accessed | tf_op | source)
XLA Modules:
  0.0 36.2 jit_solution(2825815485288197577)
XLA Ops:
  0.6 1.3 %pack.1 = (f32[8,2,64,128]{3,2,1,0:T(8,128)S(1)}, f32[6,2,32,128]{3,2,1,0:T(8,128)S(1)}, f32[106,8,128]{2,1,0:T(8,128)S(1)}, f32[106,8,128]{2,1,0:T(8,128)S(1)}, f32[11,2,32,128]{3,2,1,0:T(8,128)S(1)}) custom-call(f32[3,8,8,256]{3,2,1,0:T(8,128)} %refs_0_.2, f32[3,8,8,256]{3,2,1,0:T(8,128)} %refs_1_.2, f32[8,8,256]{2,1,0:T(8,128)} %refs_2_.2, ...), custom_call_target="tpu_custom_call" | custom-call | tf_op jit(solution)/shard_map/pack/pallas_call | solution.py:572
  2.0 2.1 %collective-permute-start = (f32[11,2,32,128]{3,2,1,0:T(8,128)S(1)}, f32[11,2,32,128]{3,2,1,0:T(8,128)S(1)}, u32[]{:S(2)}, u32[]{:S(2)}) collective-permute-start(f32[11,2,32,128]{3,2,1,0:T(8,128)S(1)} %get-tuple-element.32), channel_id=1, source_target_pairs={{0,16},{16,0},{1,17},{17,1},{2,18},{18,2},{3,19},{19,3},{4,20},{20... | collective-permute-start | bytes 1081352 | tf_op jit(solution)/shard_map/ppermute | solution.py:591
  4.1 4.0 %collective-permute-start.3 = (f32[106,8,128]{2,1,0:T(8,128)S(1)}, f32[106,8,128]{2,1,0:T(8,128)S(1)}, u32[]{:S(2)}, u32[]{:S(2)}) collective-permute-start(f32[106,8,128]{2,1,0:T(8,128)S(1)} %get-tuple-element.37), channel_id=1, source_target_pairs={{1,2},{3,4},{5,6},{7,8},{9,10},{11,12},{13,14},{2,1},{4,3},{6,5},{... | collective-permute-start | bytes 1302536 | tf_op jit(solution)/shard_map/ppermute | solution.py:586
  8.1 0.1 collective-permute-start.4
  8.1 4.0 %collective-permute-done.refs_0_.refs_3_ = f32[11,2,32,128]{3,2,1,0:T(8,128)S(1)} collective-permute-done((f32[11,2,32,128]{3,2,1,0:T(8,128)S(1)}, f32[11,2,32,128]{3,2,1,0:T(8,128)S(1)}, u32[]{:S(2)}, u32[]{:S(2)}) %collective-permute-start) | collective-permute-done | bytes 360480 | tf_op jit(solution)/shard_map/ppermute | solution.py:591
  12.2 4.5 %collective-permute-start.1 = (f32[61,8,128]{2,1,0:T(8,128)S(1)}, f32[61,8,128]{2,1,0:T(8,128)S(1)}, u32[]{:S(2)}, u32[]{:S(2)}) collective-permute-start(f32[61,8,128]{2,1,0:T(8,128)S(1)} %get-tuple-element.33), channel_id=1, source_target_pairs={{1,2},{3,4},{5,6},{7,8},{9,10},{11,12},{13,14},{2,1},{4,3},{6,5},{... | collective-permute-start | bytes 749576 | tf_op jit(solution)/shard_map/ppermute | solution.py:586
  16.8 0.1 collective-permute-start.2
  16.9 1.5 %matrix.1 = (bf16[256,240]{1,0:T(8,128)(2,1)S(1)}, bf16[128,144]{1,0:T(8,128)(2,1)S(1)}, bf16[128,192]{1,0:T(8,128)(2,1)S(1)}, bf16[128,160]{1,0:T(8,128)(2,1)S(...) custom-call(f32[48,24]{1,0:T(8,128)} %bitcast.1, ...), custom_call_target="tpu_custom_call" | custom-call | tf_op jit(solution)/shard_map/matrix/pallas_call | solution.py:545
  18.3 2.2 %collective-permute-done.3.refs_4_ = f32[106,8,128]{2,1,0:T(8,128)S(1)} collective-permute-done((f32[106,8,128]{2,1,0:T(8,128)S(1)}, f32[106,8,128]{2,1,0:T(8,128)S(1)}, u32[]{:S(2)}, u32[]{:S(2)}) %collective-permute-start.3) | collective-permute-done | bytes 434208 | tf_op jit(solution)/shard_map/ppermute | solution.py:586
  20.5 0.0 collective-permute-done.4.refs_5_
  20.5 1.7 %begin.1 = (f32[16,2,80,128]{3,2,1,0:T(8,128)S(1)}, f32[16,2,80,128]{3,2,1,0:T(8,128)S(1)}, f32[16,2,80,128]{3,2,1,0:T(8,128)S(1)}, f32[16,2,20,128]{3,2,1,0:T(8...) custom-call(f32[17,8,128]{2,1,0:T(8,128)S(1)} %get-tuple-element.25., ...), custom_call_target="tpu_custom_call" | custom-call | tf_op jit(solution)/shard_map/begin/pallas_call | solution.py:616
  22.2 1.0 %collective-permute-done.1.refs_7_ = f32[61,8,128]{2,1,0:T(8,128)S(1)} collective-permute-done((f32[61,8,128]{2,1,0:T(8,128)S(1)}, f32[61,8,128]{2,1,0:T(8,128)S(1)}, u32[]{:S(2)}, u32[]{:S(2)}) %collective-permute-start.1) | collective-permute-done | bytes 249888 | tf_op jit(solution)/shard_map/ppermute | solution.py:586
  23.2 0.0 collective-permute-done.2.refs_8_
  23.2 13.0 %steps.1 = (f32[3,8,8,256]{3,2,1,0:T(8,128)}, f32[3,8,8,256]{3,2,1,0:T(8,128)}, f32[16,2,80,128]{3,2,1,0:T(8,128)S(1)}, f32[16,2,80,128]{3,2,1,0:T(8,128)S(1)}, ...) custom-call(f32[17,8,128]{2,1,0:T(8,128)S(1)} %get-tuple-element.25., ...), custom_call_target="tpu_custom_call", output_to_operand_aliasing={{2}: (9, {}), {3}: (10, {}), {4}: (11, {}), {5}: (12, {}), ... | custom-call | tf_op jit(solution)/shard_map/steps/pallas_call | solution.py:626
  (1 shorter events, 0.0 us)
Async XLA Ops:
  2.0 10.2 %collective-permute-start = (f32[11,2,32,128]{3,2,1,0:T(8,128)S(1)}, f32[11,2,32,128]{3,2,1,0:T(8,128)S(1)}, u32[]{:S(2)}, u32[]{:S(2)}) collective-permute-start(f32[11,2,32,128]{3,2,1,0:T(8,128)S(1)} %get-tuple-element.32), channel_id=1, source_target_pairs={{0,16},{16,0},{1,17},{17,1},{2,18},{18,2},{3,19},{19,3},{4,20},{20... | collective-permute-start | bytes 1081352 | tf_op jit(solution)/shard_map/ppermute | solution.py:591
  4.1 16.5 %collective-permute-start.3 = (f32[106,8,128]{2,1,0:T(8,128)S(1)}, f32[106,8,128]{2,1,0:T(8,128)S(1)}, u32[]{:S(2)}, u32[]{:S(2)}) collective-permute-start(f32[106,8,128]{2,1,0:T(8,128)S(1)} %get-tuple-element.37), channel_id=1, source_target_pairs={{1,2},{3,4},{5,6},{7,8},{9,10},{11,12},{13,14},{2,1},{4,3},{6,5},{... | collective-permute-start | bytes 1302536 | tf_op jit(solution)/shard_map/ppermute | solution.py:586
  8.1 12.5 %collective-permute-start.4 = (f32[106,8,128]{2,1,0:T(8,128)S(1)}, f32[106,8,128]{2,1,0:T(8,128)S(1)}, u32[]{:S(2)}, u32[]{:S(2)}) collective-permute-start(f32[106,8,128]{2,1,0:T(8,128)S(1)} %get-tuple-element.38), channel_id=1, source_target_pairs={{0,1},{2,3},{4,5},{6,7},{8,9},{10,11},{12,13},{14,15},{1,0},{3,2},... | collective-permute-start | bytes 1302536 | tf_op jit(solution)/shard_map/ppermute | solution.py:586
  12.2 11.0 %collective-permute-start.1 = (f32[61,8,128]{2,1,0:T(8,128)S(1)}, f32[61,8,128]{2,1,0:T(8,128)S(1)}, u32[]{:S(2)}, u32[]{:S(2)}) collective-permute-start(f32[61,8,128]{2,1,0:T(8,128)S(1)} %get-tuple-element.33), channel_id=1, source_target_pairs={{1,2},{3,4},{5,6},{7,8},{9,10},{11,12},{13,14},{2,1},{4,3},{6,5},{... | collective-permute-start | bytes 749576 | tf_op jit(solution)/shard_map/ppermute | solution.py:586
  16.8 6.4 %collective-permute-start.2 = (f32[61,8,128]{2,1,0:T(8,128)S(1)}, f32[61,8,128]{2,1,0:T(8,128)S(1)}, u32[]{:S(2)}, u32[]{:S(2)}) collective-permute-start(f32[61,8,128]{2,1,0:T(8,128)S(1)} %get-tuple-element.34), channel_id=1, source_target_pairs={{0,1},{2,3},{4,5},{6,7},{8,9},{10,11},{12,13},{14,15},{1,0},{3,2},... | collective-permute-start | bytes 749576 | tf_op jit(solution)/shard_map/ppermute | solution.py:586
